TPU v7x, 32 devices: a whole 2x2x4 slice. The times are simulated.
32 devices in a mesh: group: 2 (over y), tp: 16 (over z, x, core).
Axes of the slice: x: 2, y: 2, z: 4, core: 2. Of those that a mesh axis runs over, the one named last changes fastest.
Arguments:
- queries: bfloat16 [2, 8, 2, 8192], P('group', None, None, 'tp'), may hold values from -24 to 24
- new_keys: bfloat16 [2, 8, 2, 1024], P('group', None, None, 'tp'), may hold values from -16 to 16
- new_values: bfloat16 [2, 8, 2, 1024], P('group', None, None, 'tp'), may hold values from -24 to 24
- key_pages: bfloat16 [2, 1024, 16, 1024], P('group', 'tp'), may hold values from -16 to 16
- value_pages: bfloat16 [2, 1024, 16, 1024], P('group', 'tp'), may hold values from -24 to 24
- page_owner: int32 [2, 1024], P('group', 'tp'), may hold values from 0 to 8, as said below
- page_fill: int32 [2, 1024], P('group', 'tp'), may hold values from 0 to 16, as said below
- target_slot: int32 [2, 8], P('group'), may hold values from 0 to 8, as said below
- out_weight: bfloat16 [8192, 8192], P(None, 'tp'), may hold values from -0.0625 to 0.0625
Outputs:
- projected: bfloat16 [2, 8, 2, 8192], P('group', None, None, 'tp')
Inputs may be any that keep to these rules, and one draw needn't show every extreme that they name: `page_owner`: the owning request slot, or 8 for a free page. Of each pair of groups g and g XOR (1) one is loaded (no free pages) and the other light; group 0 is light, and so is group 2 - 1 when 2 > 2. One device holds at most 16 pages of moving requests, and some device of every loaded group holds exactly 16. `page_fill`: 1 to 16 for a used page, 0 for a free one. `target_slot`: 8 for a request that stays. Every group has exactly one moving request; their slots in the partner group are distinct and own no pages there.
All inputs are finite; a program needn't handle non-finite values.
Results may differ from a plain program's by a relative error of at most 0.0065.
Values may be sent and summed in bfloat16 or wider, within the bound.
No kernel may reach another device: no remote copies, remote signals or barrier semaphores. Data moves between devices by JAX's collectives and lax.ppermute only.
A program may use at most 64 MiB of HBM per device.

v0:
```python
import math

import jax
import jax.numpy as jnp
from jax import lax
from jax.sharding import PartitionSpec as P

HEADS = 64
KVH = 8
HD = 128
PAGE = 16
MOVE = 1


neg_big = -1e30


def swapped(value, axis, distance):
    return lax.ppermute(value, axis, [(i, i ^ 1 << distance) for i in range(lax.axis_size(axis))])


def combined_all(part, axis, combine):
    gathered = jax.tree.map(lambda a: lax.all_gather(a, axis), part)

    def take(source):
        return jax.tree.map(lambda a: lax.dynamic_index_in_dim(a, source, 0, False), gathered)

    return lax.fori_loop(
        1, lax.axis_size(axis), lambda source, state: combine(state, take(source)), take(0)
    )


def merge_states(first, second):
    largest = jnp.maximum(first[0], second[0])
    scale_first = jnp.exp(first[0] - largest)
    scale_second = jnp.exp(second[0] - largest)
    return (
        largest,
        first[1] * scale_first + second[1] * scale_second,
        first[2] * scale_first[..., None] + second[2] * scale_second[..., None],
    )


def page_states(query_rows, key_block, value_block, owner_rows, fill_counts, row_count):
    page_count = key_block.shape[0]
    step_count = query_rows.shape[1]
    group_size = HEADS // KVH
    scale_factor = 1.0 / math.sqrt(HD)
    clipped = jnp.clip(owner_rows, 0, row_count - 1)
    query_page = jnp.take(query_rows, clipped, axis=0).reshape(
        page_count, step_count, KVH, group_size, HD
    )
    key_page = key_block.reshape(page_count, PAGE, KVH, HD)
    value_page = value_block.reshape(page_count, PAGE, KVH, HD)
    scores = (
        jnp.einsum("psgjd,ptgd->psgjt", query_page, key_page, preferred_element_type=jnp.float32)
        * scale_factor
    )
    live_token = (owner_rows < row_count)[:, None] & (
        lax.broadcasted_iota(jnp.int32, (page_count, PAGE), 1) < fill_counts[:, None]
    )
    token_mask = live_token[:, None, None, None, :]
    scores = jnp.where(token_mask, scores, neg_big)
    page_top = jnp.max(scores, axis=4).reshape(page_count, step_count * HEADS)
    member = owner_rows[None, :] == lax.broadcasted_iota(jnp.int32, (row_count, page_count), 0)
    row_top = jnp.max(jnp.where(member[:, :, None], page_top[None], neg_big), axis=1)
    top_page = jnp.take(row_top, clipped, axis=0).reshape(
        page_count, step_count, KVH, group_size, 1
    )
    weights = jnp.where(token_mask, jnp.exp(scores - top_page), 0.0).astype(jnp.bfloat16)
    weighted = jnp.einsum(
        "psgjt,ptgd->psgjd", weights, value_page, preferred_element_type=jnp.float32
    ).reshape(page_count, step_count * HEADS * HD)
    weight_sum = jnp.sum(weights.astype(jnp.float32), axis=4).reshape(
        page_count, step_count * HEADS
    )
    onehot = member.astype(jnp.float32)
    row_sum = jnp.dot(onehot, weight_sum, precision=lax.Precision.HIGHEST)
    row_acc = jnp.dot(onehot, weighted, precision=lax.Precision.HIGHEST)
    return (
        row_top.reshape(row_count, step_count, HEADS),
        row_sum.reshape(row_count, step_count, HEADS),
        row_acc.reshape(row_count, step_count, HEADS, HD),
    )


def new_token_states(query_heads, key_rows, value_rows, head_kv):
    row_count = key_rows.shape[0]
    step_count = key_rows.shape[1]
    scale_factor = 1.0 / math.sqrt(HD)
    key_heads = jnp.take(key_rows.reshape(row_count, step_count, KVH, HD), head_kv, axis=2)
    value_heads = jnp.take(
        value_rows.reshape(row_count, step_count, KVH, HD), head_kv, axis=2
    ).astype(jnp.float32)
    scores = (
        jnp.einsum("rshd,ruhd->rshu", query_heads, key_heads, preferred_element_type=jnp.float32)
        * scale_factor
    )
    causal = (
        lax.broadcasted_iota(jnp.int32, (step_count, step_count), 1)
        <= lax.broadcasted_iota(jnp.int32, (step_count, step_count), 0)
    )[None, :, None, :]
    scores = jnp.where(causal, scores, neg_big)
    largest = jnp.max(scores, axis=3)
    weights = jnp.where(causal, jnp.exp(scores - largest[..., None]), 0.0)
    return (
        largest,
        jnp.sum(weights, axis=3),
        jnp.einsum("rshu,ruhd->rshd", weights, value_heads, precision=lax.Precision.HIGHEST),
    )


def per_device(
    queries,
    new_keys,
    new_values,
    key_pages,
    value_pages,
    page_owner,
    page_fill,
    target_slot,
    out_weight,
):
    row_count = queries.shape[1]
    step_count = queries.shape[2]
    partner_bit = lax.axis_size("group").bit_length() - 2
    query_rows, key_rows, value_rows = (
        lax.all_gather(queries[0], "tp", axis=2, tiled=True),
        lax.all_gather(new_keys[0], "tp", axis=2, tiled=True),
        lax.all_gather(new_values[0], "tp", axis=2, tiled=True),
    )
    owners = page_owner[0]
    fill_counts = page_fill[0]
    slot_targets = target_slot[0]
    clipped = jnp.clip(owners, 0, row_count - 1)
    page_target = jnp.take(slot_targets, clipped)
    occupied = owners < row_count
    moving = occupied & (page_target < row_count)
    partner_targets = swapped(slot_targets, "group", partner_bit)
    slot_ids = lax.broadcasted_iota(jnp.int32, (row_count,), 0)
    mover_ids = lax.broadcasted_iota(jnp.int32, (MOVE, row_count), 0)
    their_moving = partner_targets < row_count
    their_rank = jnp.cumsum(their_moving.astype(jnp.int32)) - 1
    their_pick = their_moving[None, :] & (their_rank[None, :] == mover_ids)
    pick_rows = jnp.sum(their_pick.astype(jnp.int32) * partner_targets[None, :], axis=1)
    pick_valid = jnp.any(their_pick, axis=1)
    send_pick = pick_valid[:, None] & (pick_rows[:, None] == slot_ids[None, :])
    sent_queries = jnp.einsum(
        "mr,rsd->msd",
        send_pick.astype(jnp.bfloat16),
        query_rows,
        preferred_element_type=jnp.float32,
    ).astype(jnp.bfloat16)
    arrived_queries = swapped(sent_queries, "group", partner_bit)
    own_moving = slot_targets < row_count
    own_rank = jnp.cumsum(own_moving.astype(jnp.int32)) - 1
    page_rank = jnp.take(own_rank, clipped)
    local_rows = jnp.where(
        occupied, jnp.where(moving, row_count + page_rank, owners), row_count + MOVE
    )
    joined = page_states(
        jnp.concatenate([query_rows, arrived_queries], axis=0),
        key_pages[0],
        value_pages[0],
        local_rows,
        fill_counts,
        row_count + MOVE,
    )
    own_part = tuple((member_array[:row_count] for member_array in joined))
    theirs = tuple((member_array[row_count:] for member_array in joined))
    returned = swapped((theirs[0], theirs[1], theirs[2]), "group", partner_bit)
    placement_table = send_pick.astype(jnp.float32)
    placed_any = jnp.any(send_pick, axis=0)
    placed_max = jnp.where(
        placed_any[:, None, None],
        jnp.einsum("mr,msh->rsh", placement_table, returned[0], precision=lax.Precision.HIGHEST),
        neg_big,
    )
    placed_sum = jnp.einsum(
        "mr,msh->rsh", placement_table, returned[1], precision=lax.Precision.HIGHEST
    )
    placed_acc = jnp.einsum(
        "mr,mshd->rshd", placement_table, returned[2], precision=lax.Precision.HIGHEST
    )
    states = merge_states(own_part, (placed_max, placed_sum, placed_acc))
    head_kv_all = lax.broadcasted_iota(jnp.int32, (HEADS,), 0) // (HEADS // KVH)
    query_heads = query_rows.reshape(row_count, step_count, HEADS, HD)
    combined = combined_all((states[0], states[1], states[2]), "tp", merge_states)
    new_terms = new_token_states(query_heads, key_rows, value_rows, head_kv_all)
    finished = merge_states(combined, new_terms)
    attention = (
        (finished[2] / finished[1][..., None])
        .astype(jnp.bfloat16)
        .reshape(row_count * step_count, HEADS * HD)
    )
    projected = jnp.dot(attention, out_weight, preferred_element_type=jnp.float32).astype(
        jnp.bfloat16
    )
    return projected.reshape(1, row_count, step_count, out_weight.shape[1])


def solution(mesh):
    placed = (
        P("group", None, None, "tp"),
        P("group", None, None, "tp"),
        P("group", None, None, "tp"),
        P("group", "tp", None, None),
        P("group", "tp", None, None),
        P("group", "tp"),
        P("group", "tp"),
        P("group", None),
        P(None, "tp"),
    )
    return jax.shard_map(
        per_device,
        mesh=mesh,
        in_specs=placed,
        out_specs=P("group", None, None, "tp"),
        check_vma=False,
    )
```

profile of v0, /device:TPU:0, one launch (start us, length us, event | category | flops | bytes accessed | tf_op | source)
XLA Modules:
  0.0 223.6 jit_solution(14644763378011074717)
XLA Ops:
  6.5 3.0 %collective-permute-start = (s32[8]{0:T(128)}, s32[8]{0:T(128)S(1)}, u32[]{:S(2)}, u32[]{:S(2)}) collective-permute-start(s32[8]{0:T(128)} %bitcast.168), channel_id=1, source_target_pairs={{0,16},{16,0},{1,17},{17,1},{2,18},{18,2},{3,19},{19,3},{4,20},{20... | collective-permute-start | bytes 104 | tf_op jit(solution)/shard_map/ppermute | solution.py:19
  9.5 0.7 fusion.42
  10.2 1.6 fusion.52
  12.7 10.6 %broadcast_compare_fusion = (pred[64]{0:T(512)(128)(4,1)S(1)}, s32[64]{0:T(128)S(1)}) fusion(s32[]{:T(128)} %bitcast.22, s32[]{:T(128)} %bitcast.21, s32[]{:T(128)} %bitcast.20, s32[]{:T(128)} %bitcast.19, s32[]{:T(128)} %bitcast.18, s32[]{:T(128)} %bitcast.17, s32[]{:T(128)} %bitcast.16, s32[]{:T(128)} %bitcast.15, s32[]{:T(128)} %bitcast.12, s32[]{:T(128)} %bitcast.11, ...), kind=kLoop, calls=%fused_computation.120 | loop fusion | flops 2368 | bytes 640 | tf_op jit(solution)/shard_map/lt | solution.py:59
  23.4 22.6 %all-gather = bf16[1,8,2,8192]{3,2,1,0:T(2,128)(2,1)S(1)} all-gather(bf16[1,8,2,512]{3,2,1,0:T(2,128)(2,1)} %param.15), channel_id=2, replica_groups=mesh['group'=2,'tp'=16] {'tp'}, dimensions={3}, use_global_device_ids=true | all-gather | bytes 278528 | tf_op jit(solution)/shard_map/all_gather | solution.py:128
  45.9 2.4 %copy.149 = bf16[128,8,8,128]{3,2,1,0:T(8,128)(2,1)S(1)} copy(bf16[128,8,8,128]{3,1,2,0:T(8,128)(2,1)} %bitcast.155) | data formatting | bytes 4194304
  48.3 1.5 bitcast_bitcast_fusion.1
  50.4 1.5 bitcast_bitcast_fusion
  52.2 0.7 select_reduce_fusion.1
  53.6 1.3 compare_and_fusion.2
  55.9 1.3 fusion.43
  57.3 2.1 collective-permute-done.1
  59.7 6.1 %gather_fusion = bf16[64,2,8192]{2,1,0:T(2,128)(2,1)S(1)} fusion(bf16[9,2,8192]{2,1,0:T(2,128)(2,1)S(1)} %pad_maximum_fusion, s32[1024]{0:T(1024)S(1)} %pad_clamp_fusion.1), kind=kCustom, calls=%fused_computation.2 | custom fusion | bytes 4194560 | tf_op jit(solution)/shard_map/jit(_take)/gather | solution.py:50
  65.8 2.9 %gather.19 = bf16[64,2,8,8,128]{4,3,2,1,0:T(8,128)(2,1)} reshape(bf16[64,2,8192]{2,1,0:T(2,128)(2,1)S(1)} %gather_fusion) | data formatting | bytes 4194304 | tf_op jit(solution)/shard_map/jit(_take)/gather | solution.py:50
  68.7 5.8 %bitcast_reduce_fusion = (f32[64,2,8,8]{3,1,2,0:T(2,128)S(1)}, f32[64,8,2,8,16]{4,3,2,1,0:T(8,128)}) fusion(pred[64,16]{1,0:T(8,128)(4,1)S(1)} %fusion.29, bf16[64,16,8,128,1]{3,2,1,0,4:T(8,128)(2,1)} %bitcast_bitcast_fusion.1, bf16[64,2,8,8,128]{4,3,2,1,0:T(8,128)(2,1)} %gather.19, pred[64]{0:T(512)(128)(4,1)S(1)} %get-tuple-element.215), kind=kOutput, calls=%fused_computation.16 | convolution fusion | flops 34988032 | bytes 4752448 | tf_op jit(solution)/shard_map/psgjd,ptgd->psgjt/dot_general | solution.py:56
  76.8 4.9 %convert_reduce_fusion = f32[64,2,8,8]{3,1,2,0:T(2,128)S(1)} fusion(f32[64,2,8,8]{3,1,2,0:T(2,128)S(1)} %copy.112, f32[64,8,2,8,16]{4,3,2,1,0:T(8,128)} %get-tuple-element.238, pred[64,16]{1,0:T(8,128)(4,1)S(1)} %fusion.29), kind=kLoop, calls=%fused_computation.20 | loop fusion | flops 909312 | bytes 590848 | tf_op jit(solution)/shard_map/reduce_sum | solution.py:74
  82.3 1.5 collective-permute-start.3
  83.8 4.2 %convolution_bitcast_fusion = f32[64,2,8,8,128]{4,3,1,2,0:T(8,128)S(1)} fusion(bf16[64,16,8,128,1]{3,2,1,0,4:T(8,128)(2,1)S(1)} %copy-done.1, f32[64,8,2,8,16]{4,3,2,1,0:T(8,128)} %get-tuple-element.238, f32[64,2,8,8]{3,1,2,0:T(2,128)S(1)} %copy.112, pred[64,16]{1,0:T(8,128)(4,1)S(1)} %fusion.29), kind=kOutput, calls=%fused_computation.22 | convolution fusion | flops 34209792 | bytes 6849536 | tf_op jit(solution)/shard_map/psgjt,ptgd->psgjd/dot_general | solution.py:71
  88.5 3.8 %fusion.3 = f32[9,16384]{1,0:T(8,128)S(1)} fusion(f32[8,8,128,128]{3,2,1,0:T(8,128)S(1)} %bitcast.149, s32[64]{0:T(128)S(1)} %get-tuple-element.214), kind=kOutput, calls=%fused_computation.12 | convolution fusion | flops 113246784 | bytes 4784384 | tf_op jit(solution)/shard_map/dot_general | solution.py:79
  93.3 3.6 %collective-permute-done.4 = f32[1,2,64,128]{3,2,1,0:T(8,128)S(1)} collective-permute-done((f32[1,2,64,128]{3,2,1,0:T(8,128)S(1)}, f32[1,2,64,128]{3,2,1,0:T(8,128)S(1)}, u32[]{:S(2)}, u32[]{:S(2)}) %collective-permute-start.4) | collective-permute-done | bytes 65568 | tf_op jit(solution)/shard_map/ppermute | solution.py:19
  96.9 1.2 fusion.19
  98.3 20.6 %all-gather.5 = bf16[1,8,2,1024]{1,2,0,3:T(2,128)(2,1)S(1)} all-gather(bf16[1,8,2,64]{1,2,0,3:T(2,128)(2,1)S(1)} %copy.125), channel_id=7, replica_groups=mesh['group'=2,'tp'=16] {'tp'}, dimensions={3}, use_global_device_ids=true | all-gather | bytes 34816 | tf_op jit(solution)/shard_map/all_gather | solution.py:130
  119.2 22.3 %all-gather.4 = bf16[1,8,2,1024]{1,2,0,3:T(2,128)(2,1)S(1)} all-gather(bf16[1,8,2,64]{1,2,0,3:T(2,128)(2,1)S(1)} %copy.117), channel_id=6, replica_groups=mesh['group'=2,'tp'=16] {'tp'}, dimensions={3}, use_global_device_ids=true | all-gather | bytes 34816 | tf_op jit(solution)/shard_map/all_gather | solution.py:129
  141.9 0.7 gather_fusion.3
  142.5 0.7 gather_fusion.2
  143.4 1.1 fusion.54
  144.6 0.9 fusion.30
  145.7 2.4 %fusion.24 = f32[8,64,128,2]{2,3,1,0:T(2,128)S(1)} fusion(bf16[8,2,64,128]{3,0,1,2:T(8,128)(2,1)S(1)} %get-tuple-element.234, f32[8,2,64,2]{1,3,2,0:T(2,128)S(1)} %get-tuple-element.236, pred[2,2]{0,1:T(4,128)(4,1)S(1)} %iota_compare_fusion.4, f32[8,2,64]{1,2,0:T(8,128)S(1)} %get-tuple-element.235), kind=kOutput, calls=%fused_computation.50 | convolution fusion | flops 3149824 | bytes 798724 | tf_op jit(solution)/shard_map/rshu,ruhd->rshd/dot_general | solution.py:109
  148.1 18.7 %all-gather.2 = f32[128,2,64]{2,1,0:T(2,128)S(1)} all-gather(f32[8,2,64]{2,1,0:T(2,128)S(1)} %get-tuple-element.209), channel_id=4, replica_groups=mesh['group'=2,'tp'=16] {'tp'}, dimensions={0}, use_global_device_ids=true | all-gather | bytes 69632 | tf_op jit(solution)/shard_map/all_gather | solution.py:23
  166.8 19.0 %all-gather.1 = f32[128,2,64]{2,1,0:T(2,128)S(1)} all-gather(f32[8,2,64]{2,1,0:T(2,128)S(1)} %get-tuple-element.212), channel_id=3, replica_groups=mesh['group'=2,'tp'=16] {'tp'}, dimensions={0}, use_global_device_ids=true | all-gather | bytes 69632 | tf_op jit(solution)/shard_map/all_gather | solution.py:23
  185.8 1.1 slice.104
  186.9 24.2 %while.19 = (s32[]{:T(128)}, f32[8,2,64]{2,1,0:T(2,128)S(1)}, f32[8,2,64]{2,1,0:T(2,128)S(1)}, f32[8,2,64,128]{3,2,1,0:T(8,128)S(1)}, f32[16,8,2,64]{3,2,1,0:T(2...) while((s32[]{:T(128)}, f32[8,2,64]{2,1,0:T(2,128)S(1)}, ...), condition=%wide.region_8.10_spmd, body=%wide.region_7.9_spmd.sunk | while | flops 399365 | bytes 1613967 | solution.py:28
  186.9 1.5 fusion.60
  188.6 1.5 fusion.60
  190.2 1.5 fusion.60
  191.8 1.5 fusion.60
  193.4 1.5 fusion.60
  195.0 1.5 fusion.60
  196.6 1.5 fusion.60
  198.2 1.5 fusion.60
  199.8 1.5 fusion.60
  201.4 1.5 fusion.60
  203.1 1.5 fusion.60
  204.7 1.5 fusion.60
  206.3 1.5 fusion.60
  207.9 1.5 fusion.60
  209.5 1.5 fusion.60
  211.6 4.6 %convolution_convert_fusion = bf16[16,512]{1,0:T(8,128)(2,1)S(1)} fusion(bf16[8192,512]{1,0:T(8,128)(2,1)} %param.23, bf16[2,8,64,128]{3,2,1,0:T(8,128)(2,1)S(1)} %bitcast.154), kind=kOutput, calls=%fused_computation.33 | convolution fusion | flops 134225920 | bytes 8667136 | tf_op jit(solution)/shard_map/dot_general | solution.py:196
  (88 shorter events, 11.3 us)
Async XLA Ops:
  6.5 179.3 %all-gather.8.cloned.1.call-start = ((), (), s32[]{:S(2)}) async-start(), calls=%async_computation | async-start | bytes 8912896 | tf_op jit(solution)/shard_map/all_gather | solution.py:23
  6.5 45.5 %collective-permute-start = (s32[8]{0:T(128)}, s32[8]{0:T(128)S(1)}, u32[]{:S(2)}, u32[]{:S(2)}) collective-permute-start(s32[8]{0:T(128)} %bitcast.168), channel_id=1, source_target_pairs={{0,16},{16,0},{1,17},{17,1},{2,18},{18,2},{3,19},{19,3},{4,20},{20... | collective-permute-start | bytes 104 | tf_op jit(solution)/shard_map/ppermute | solution.py:19
  45.9 3.9 %copy-start = (bf16[1,64,16,1024]{3,2,1,0:T(8,128)(2,1)S(1)}, bf16[1,64,16,1024]{3,2,1,0:T(8,128)(2,1)}, u32[]{:S(2)}) copy-start(bf16[1,64,16,1024]{3,2,1,0:T(8,128)(2,1)} %param.19) | copy-start | bytes 6291460
  49.8 2.1 copy-start.4
  55.4 4.0 %collective-permute-start.1 = (bf16[1,2,8192]{2,1,0:T(2,128)(2,1)S(1)}, bf16[1,2,8192]{2,1,0:T(2,128)(2,1)S(1)}, u32[]{:S(2)}, u32[]{:S(2)}) collective-permute-start(bf16[1,2,8192]{2,1,0:T(2,128)(2,1)S(1)} %copy.193), channel_id=1, source_target_pairs={{0,16},{16,0},{1,17},{17,1},{2,18},{18,2},{3,19},{19,3},{4,20},{20... | collective-permute-start | bytes 98312 | tf_op jit(solution)/shard_map/ppermute | solution.py:19
  74.5 9.3 %copy-start.1 = (bf16[64,16,8,128,1]{3,2,1,0,4:T(8,128)(2,1)S(1)}, bf16[64,16,8,128,1]{3,2,1,0,4:T(8,128)(2,1)}, u32[]{:S(2)}) copy-start(bf16[64,16,8,128,1]{3,2,1,0,4:T(8,128)(2,1)} %bitcast_bitcast_fusion) | copy-start | bytes 6291460
  75.7 17.5 %collective-permute-start.2 = (f32[1,2,64]{2,1,0:T(2,128)S(1)}, f32[1,2,64]{2,1,0:T(2,128)S(1)}, u32[]{:S(2)}, u32[]{:S(2)}) collective-permute-start(f32[1,2,64]{2,1,0:T(2,128)S(1)} %slice.42), channel_id=1, source_target_pairs={{0,16},{16,0},{1,17},{17,1},{2,18},{18,2},{3,19},{19,3},{4,20},{20... | collective-permute-start | bytes 1544 | tf_op jit(solution)/shard_map/ppermute | solution.py:19
  82.3 10.9 %collective-permute-start.3 = (f32[1,2,64]{2,1,0:T(2,128)S(1)}, f32[1,2,64]{2,1,0:T(2,128)S(1)}, u32[]{:S(2)}, u32[]{:S(2)}) collective-permute-start(f32[1,2,64]{2,1,0:T(2,128)S(1)} %slice.46), channel_id=1, source_target_pairs={{0,16},{16,0},{1,17},{17,1},{2,18},{18,2},{3,19},{19,3},{4,20},{20... | collective-permute-start | bytes 1544 | tf_op jit(solution)/shard_map/ppermute | solution.py:19
  88.5 9.6 %copy-start.2 = (bf16[1,8,2,64]{3,2,1,0:T(2,128)(2,1)S(1)}, bf16[1,8,2,64]{3,2,1,0:T(2,128)(2,1)}, u32[]{:S(2)}) copy-start(bf16[1,8,2,64]{3,2,1,0:T(2,128)(2,1)} %param.16) | copy-start | bytes 6148
  88.5 9.7 %copy-start.3 = (bf16[1,8,2,64]{3,2,1,0:T(2,128)(2,1)S(1)}, bf16[1,8,2,64]{3,2,1,0:T(2,128)(2,1)}, u32[]{:S(2)}) copy-start(bf16[1,8,2,64]{3,2,1,0:T(2,128)(2,1)} %param.17) | copy-start | bytes 6148
  92.6 4.3 %collective-permute-start.4 = (f32[1,2,64,128]{3,2,1,0:T(8,128)S(1)}, f32[1,2,64,128]{3,2,1,0:T(8,128)S(1)}, u32[]{:S(2)}, u32[]{:S(2)}) collective-permute-start(f32[1,2,64,128]{3,2,1,0:T(8,128)S(1)} %bitcast.167), channel_id=1, source_target_pairs={{0,16},{16,0},{1,17},{17,1},{2,18},{18,2},{3,19},{19,3},{4,20},{20... | collective-permute-start | bytes 196616 | tf_op jit(solution)/shard_map/ppermute | solution.py:19
Sparse Core Ops, SparseCore 0:
  98.2 73.7 all-gather.7
where the time goes:
time: 225 us; the launch traced here: 224 us
  blocking collectives  103 us (46%)
  other arithmetic  48 us (21%)
  local copies, waits for them, and re-layouts  24.2 us (11%)
  matrix products  22.4 us (10%)
  between operations  13.8 us (6%)
  starting transfers between devices  6.19 us (3%)
  waiting for transfers between devices  5.66 us (3%)
    all_gather x2, blocking collectives, combined_all(): gathered = jax.tree.map(lambda a: lax.all_gather(a, axis), part)  37.7 us
    add x16, other arithmetic, merge_states(): first[2] * scale_first[..., None] + second[2] * scale_second[..., None]  24.4 us
    all_gather x1, blocking collectives, per_device(): lax.all_gather(queries[0], 'tp', axis=2, tiled=True)  22.6 us
    all_gather x1, blocking collectives, per_device(): lax.all_gather(new_keys[0], 'tp', axis=2, tiled=True)  22.3 us
    all_gather x1, blocking collectives, per_device(): lax.all_gather(new_values[0], 'tp', axis=2, tiled=True)  20.6 us
    lt x1, other arithmetic, page_states(): owner_rows < row_count  10.6 us
    gather x2, local copies, waits for them, and re-layouts, page_states(): jnp.take(query_rows, clipped, axis=0)  8.91 us
    ppermute x5, starting transfers between devices, swapped(): lax.ppermute(value, axis, [(i, i ^ 1 << distance) for i in range(lax.axis...  6.19 us
  transfers between devices with their start and end apart: 6, of which 2 were waited for; matrix products, arithmetic and copies ran while one was open for 19% of the time, Pallas kernels for 0%

commit v1 on v0

v1 whole, which is shorter than its diff:
```python
import math

import jax
import jax.numpy as jnp
from jax import lax
from jax.experimental import pallas as pl
from jax.experimental.pallas import tpu as pltpu
from jax.sharding import PartitionSpec as P

HEADS = 64
KVH = 8
HD = 128
PAGE = 16
NEG = -1e30
FLOOR = -1e29
SCALE = 1.0 / math.sqrt(HD) * math.log2(math.e)
MOVED_LANE = 64
GS = HEADS // KVH


def dot(a, b, contract):
    return lax.dot_general(a, b, ((contract), ((), ())), preferred_element_type=jnp.float32)


def iota(shape, axis):
    return lax.broadcasted_iota(jnp.int32, shape, axis)


def attend_kernel(
    chips, info, slots, owner, fill, own, other, keys, values, out, bias_own, bias_moved
):
    row_steps = own.shape[1]
    rows = slots.shape[0]
    steps = row_steps // rows
    features = HEADS // (2 * chips) * HD
    local_heads = features // HD
    kv_part = (own.shape[2] - features) // 2
    per_kv = chips // KVH
    tokens = keys.shape[0]
    half_rs = row_steps // 2
    half = info[0]
    core = info[1]
    first = info[2]
    mover = jnp.int32(0)
    target = jnp.int32(0)
    for r in range(rows):
        leaves = slots[r] < rows
        mover = jnp.where(leaves, r, mover)
        target = jnp.where(leaves, slots[r], target)

    pages = owner.shape[1]
    spread = (iota((pages, tokens), 1) // PAGE == iota((pages, tokens), 0)).astype(jnp.bfloat16)
    table = jnp.concatenate([owner[...], fill[...]], axis=0).astype(jnp.float32)
    table = jnp.concatenate([table] * 4, axis=0).astype(jnp.bfloat16)
    by_token = dot(table, spread, ((1,), (0,)))
    owner_tok = by_token[0:1].astype(jnp.int32)
    fill_tok = by_token[1:2].astype(jnp.int32)
    live = iota((1, tokens), 1) % PAGE < fill_tok
    token_row = jnp.where(live, owner_tok, rows)
    stay_row = jnp.where(token_row == mover, rows, token_row)
    bias_own[...] = jnp.where(iota((row_steps, tokens), 0) // steps == stay_row, 0.0, NEG)
    bias_moved[...] = jnp.broadcast_to(jnp.where(token_row == mover, 0.0, NEG), bias_moved.shape)

    rs_ids = iota((row_steps, row_steps), 0)
    new_ids = iota((row_steps, row_steps), 1)
    new_live = (rs_ids // steps == new_ids // steps) & (new_ids % steps <= rs_ids % steps)
    bias_new = jnp.where(new_live & (first == 1), 0.0, NEG)
    moved_rows = GS * steps
    wide = GS * row_steps
    pick_ids = iota((moved_rows, wide), 0)
    pick = (
        iota((moved_rows, wide), 1)
        == (pick_ids // steps) * row_steps + target * steps + pick_ids % steps
    ).astype(jnp.bfloat16)
    lane = iota((half_rs, HD), 1)
    target_f = target.astype(jnp.float32)

    def per_head(g, carry):
        tiles, partner_tiles, new_k, new_v = [], [], [], []
        for source in (own, other):
            for kl in range(per_kv):
                mine = source[half * chips + g * per_kv + kl]
                theirs = source[(1 - half) * chips + g * per_kv + kl]
                for j in range(local_heads):
                    tiles.append(mine[:, j * HD : (j + 1) * HD])
                    partner_tiles.append(theirs[:, j * HD : (j + 1) * HD])
                new_k.append(mine[:, features : features + kv_part])
                new_v.append(mine[:, features + kv_part :])

        def in_order(parts):
            mine, theirs = parts[:per_kv], parts[per_kv:]
            a = [x for pair in zip(mine, theirs) for x in pair]
            b = [x for pair in zip(theirs, mine) for x in pair]
            return jnp.where(
                core == 0,
                jnp.concatenate(a, axis=1).astype(jnp.float32),
                jnp.concatenate(b, axis=1).astype(jnp.float32),
            ).astype(jnp.bfloat16)

        moved_q = dot(pick, jnp.concatenate(partner_tiles, axis=0), ((1,), (0,)))
        q = jnp.concatenate(tiles + [moved_q.astype(jnp.bfloat16)], axis=0)
        at = pl.ds(pl.multiple_of(g * HD, HD), HD)
        k = keys[:, at]
        v = values[:, at]
        scores = dot(q, k, ((1,), (1,))) * SCALE
        bias = jnp.concatenate([bias_own[...]] * GS + [bias_moved[...]], axis=0)
        scores = scores + bias
        new_scores = dot(q[:wide], in_order(new_k), ((1,), (1,))) * SCALE
        new_scores = new_scores + jnp.concatenate([bias_new] * GS, axis=0)
        new_scores = jnp.concatenate(
            [new_scores, jnp.full((moved_rows, row_steps), NEG, jnp.float32)], axis=0
        )
        top = jnp.maximum(
            jnp.max(scores, axis=1, keepdims=True), jnp.max(new_scores, axis=1, keepdims=True)
        )
        top = jnp.maximum(top, FLOOR).astype(jnp.bfloat16).astype(jnp.float32)
        p = jnp.exp2(scores - top).astype(jnp.bfloat16)
        pn = jnp.exp2(new_scores - top).astype(jnp.bfloat16)
        total = jnp.sum(p.astype(jnp.float32), axis=1, keepdims=True) + jnp.sum(
            pn.astype(jnp.float32), axis=1, keepdims=True
        )
        acc = dot(p, v, ((1,), (0,))) + dot(pn, in_order(new_v), ((1,), (0,)))
        high = total.astype(jnp.bfloat16).astype(jnp.float32)
        low = total - high

        for side in range(2):
            for kl in range(per_kv):
                dest = 2 * (g * per_kv + kl) + jnp.where(side == 0, core, 1 - core)
                t0 = (side * per_kv + kl) * local_heads
                at_moved = slice(wide + t0 * steps, wide + (t0 + local_heads) * steps)
                moved_acc = acc[at_moved]
                short = half_rs - local_heads * steps

                def filled(x):
                    if short == 0:
                        return x
                    return jnp.concatenate([x, jnp.zeros((short, x.shape[1]), x.dtype)], axis=0)

                for h in range(2):
                    parts = [
                        acc[(t0 + j) * row_steps + h * half_rs :][:half_rs]
                        for j in range(local_heads)
                    ]
                    aux = jnp.where(lane == MOVED_LANE, filled(top[at_moved]), 0.0)
                    aux = jnp.where(lane == MOVED_LANE + 1, filled(high[at_moved]), aux)
                    aux = jnp.where(lane == MOVED_LANE + 2, filled(low[at_moved]), aux)
                    aux = jnp.where(lane == MOVED_LANE + 3, target_f, aux)
                    for j in range(local_heads):
                        rows_at = slice(
                            (t0 + j) * row_steps + h * half_rs,
                            (t0 + j) * row_steps + (h + 1) * half_rs,
                        )
                        aux = jnp.where(lane == j, top[rows_at], aux)
                        aux = jnp.where(lane == local_heads + j, high[rows_at], aux)
                        aux = jnp.where(lane == 2 * local_heads + j, low[rows_at], aux)
                    block = jnp.concatenate(parts + [filled(moved_acc), aux], axis=0)
                    out[h, dest] = block.astype(jnp.bfloat16)
        return carry

    lax.fori_loop(0, KVH, per_head, 0)


def reduce_kernel(chips, steps, info, parts, out):
    sources = 2 * chips
    half_rs = out.shape[2]
    local_heads = out.shape[3] // HD
    half = info[0]
    span = half_rs * local_heads
    row_ids = iota((half_rs, 1), 0)
    for g in range(2):
        blocks = [parts[(1 - g) * sources + t].astype(jnp.float32) for t in range(sources)]
        aux = [b[span + half_rs :] for b in blocks]
        column = [a[:, MOVED_LANE : MOVED_LANE + 1] for a in aux]
        top = column[0]
        for c in column[1:]:
            top = jnp.maximum(top, c)
        moved_sum = jnp.zeros((half_rs, 1), jnp.float32)
        moved_acc = jnp.zeros((half_rs, HD), jnp.float32)
        for t in range(sources):
            w = jnp.exp2(column[t] - top)
            a = aux[t]
            moved_sum += w * (
                a[:, MOVED_LANE + 1 : MOVED_LANE + 2] + a[:, MOVED_LANE + 2 : MOVED_LANE + 3]
            )
            moved_acc += w * blocks[t][span : span + half_rs]
        moved_top = top
        slot = aux[0][:, MOVED_LANE + 3 : MOVED_LANE + 4]
        mine = (half_rs // steps * half + row_ids // steps).astype(jnp.float32) == slot
        blocks = [parts[g * sources + t].astype(jnp.float32) for t in range(sources)]
        aux = [b[span + half_rs :] for b in blocks]
        done = []
        for j in range(local_heads):

            def placed(x):
                y = jnp.broadcast_to(x[j * steps : j * steps + 1], (half_rs, x.shape[1]))
                for s in range(1, steps):
                    z = jnp.broadcast_to(x[j * steps + s : j * steps + s + 1], y.shape)
                    y = jnp.where(row_ids % steps == s, z, y)
                return y

            m_in = jnp.where(mine, placed(moved_top), FLOOR)
            column = [a[:, j : j + 1] for a in aux]
            top = m_in
            for c in column:
                top = jnp.maximum(top, c)
            w = jnp.where(mine, jnp.exp2(m_in - top), 0.0)
            total = w * placed(moved_sum)
            acc = w * placed(moved_acc)
            for t in range(sources):
                w = jnp.exp2(column[t] - top)
                a = aux[t]
                total += w * (
                    a[:, local_heads + j : local_heads + j + 1]
                    + a[:, 2 * local_heads + j : 2 * local_heads + j + 1]
                )
                acc += w * blocks[t][j * half_rs : (j + 1) * half_rs]
            done.append(acc / total)
        result = jnp.concatenate(done, axis=1).astype(jnp.bfloat16)
        for k in range(chips):
            out[g, k] = result


def project_kernel(chips, info, own, other, weight, out):
    core = info[1]
    acc = None
    for side, source in enumerate((own, other)):
        which = core if side == 0 else 1 - core
        for k in range(chips):
            x = jnp.concatenate([source[k], source[chips + k]], axis=0)
            part = dot(x, weight[2 * k + which], ((1,), (0,)))
            acc = part if acc is None else acc + part
    out[...] = acc.astype(jnp.bfloat16)


SMEM = pl.BlockSpec(memory_space=pltpu.SMEM)
VMEM = pl.BlockSpec(memory_space=pltpu.VMEM)


def per_device_of(groups, width):
    chips = width // 2
    apart = groups // 2
    same_core = [
        [(g + h * apart) * width + 2 * k + c for h in range(2) for k in range(chips)]
        for g in range(apart)
        for c in range(2)
    ]
    paired = [
        [(g + h * apart) * width + t for h in range(2) for t in range(width)] for g in range(apart)
    ]
    across = [(t, t ^ 1) for t in range(width)]
    both = ("group", "tp")

    def exchange(x, members):
        return lax.all_to_all(x, both, 0, 0, axis_index_groups=members)

    def per_device(
        queries,
        new_keys,
        new_values,
        key_pages,
        value_pages,
        page_owner,
        page_fill,
        target_slot,
        out_weight,
    ):
        rows, steps, features = queries.shape[1:]
        local_heads = features // HD
        row_steps = rows * steps
        half_rs = row_steps // 2
        pages = key_pages.shape[1]
        tokens = pages * PAGE
        place = lax.axis_index("tp")
        half = lax.axis_index("group") // apart
        info = jnp.stack([half, place % 2, (place == 0).astype(jnp.int32)]).astype(jnp.int32)

        packed = jnp.concatenate([queries[0], new_keys[0], new_values[0]], axis=2)
        packed = packed.reshape(1, row_steps, packed.shape[2])
        sent = jnp.broadcast_to(packed, (2 * chips,) + packed.shape[1:])
        own = exchange(sent, same_core)
        other = lax.ppermute(own, "tp", across)

        block_rows = half_rs * local_heads + 2 * half_rs
        states = pl.pallas_call(
            lambda *refs: attend_kernel(chips, *refs),
            out_shape=jax.ShapeDtypeStruct((2, width, block_rows, HD), jnp.bfloat16),
            in_specs=[SMEM, SMEM] + [VMEM] * 6,
            out_specs=VMEM,
            scratch_shapes=[
                pltpu.VMEM((row_steps, tokens), jnp.float32),
                pltpu.VMEM((GS * steps, tokens), jnp.float32),
            ],
            name="attend",
        )(
            info,
            target_slot[0],
            page_owner,
            page_fill,
            own,
            other,
            key_pages.reshape(tokens, key_pages.shape[3]),
            value_pages.reshape(tokens, value_pages.shape[3]),
        )
        arrived = exchange(states.reshape(2 * width, block_rows, HD), paired)
        finished = pl.pallas_call(
            lambda *refs: reduce_kernel(chips, steps, *refs),
            out_shape=jax.ShapeDtypeStruct((2, chips, half_rs, features), jnp.bfloat16),
            in_specs=[SMEM, VMEM],
            out_specs=VMEM,
            name="reduce",
        )(info, arrived)
        own = exchange(finished.reshape(2 * chips, half_rs, features), same_core)
        other = lax.ppermute(own, "tp", across)
        projected = pl.pallas_call(
            lambda *refs: project_kernel(chips, *refs),
            out_shape=jax.ShapeDtypeStruct((row_steps, out_weight.shape[1]), jnp.bfloat16),
            in_specs=[SMEM, VMEM, VMEM, VMEM],
            out_specs=VMEM,
            name="project",
        )(info, own, other, out_weight.reshape(width, features, out_weight.shape[1]))
        return projected.reshape(1, rows, steps, out_weight.shape[1])

    return per_device


def solution(mesh):
    placed = (
        P("group", None, None, "tp"),
        P("group", None, None, "tp"),
        P("group", None, None, "tp"),
        P("group", "tp", None, None),
        P("group", "tp", None, None),
        P("group", "tp"),
        P("group", "tp"),
        P("group", None),
        P(None, "tp"),
    )
    return jax.shard_map(
        per_device_of(mesh.shape["group"], mesh.shape["tp"]),
        mesh=mesh,
        in_specs=placed,
        out_specs=P("group", None, None, "tp"),
        check_vma=False,
    )
```

time: 225 us -> 74.5 us (0.33)
  blocking collectives: 103 us -> 47.1 us
  other arithmetic: 48 us -> 1.46 us
  matrix products: 22.4 us -> 0 us
  local copies, waits for them, and re-layouts: 24.2 us -> 3.47 us
  Pallas kernels: 0 us -> 19.5 us
  between operations: 13.8 us -> 0.02 us
  starting transfers between devices: 6.19 us -> 0.01 us
  waiting for transfers between devices: 5.66 us -> 2.29 us
    all_gather x5 -> x0, blocking collectives: 103 us -> none  [the longest x2 37.7 us: combined_all(): gathered = jax.tree.map(lambda a: lax.all_gather(a, axis), part)]
    all_to_all x0 -> x3, blocking collectives: none -> 47.1 us  [exchange(): return lax.all_to_all(x, both, 0, 0, axis_index_groups=members)]
    add x33 -> x0, other arithmetic: 25.1 us -> none  [the longest x16 24.4 us: merge_states(): first[2] * scale_first[..., None] + second[2] * scale_second[..., None]]
    dot_general x8 -> x0, matrix products: 22.4 us -> none  [the longest x1 5.79 us: page_states(): jnp.einsum('psgjd,ptgd->psgjt', query_page, key_page, preferred_element_t...]
    pallas_call x0 -> x3, Pallas kernels: none -> 19.5 us  [the longest x1 8.93 us: per_device(): pl.pallas_call(lambda *refs: attend_kernel(chips, *refs), out_shape=jax.S...]
    gather x8 -> x0, local copies, waits for them, and re-layouts: 13.2 us -> none  [the longest x2 8.91 us: page_states(): jnp.take(query_rows, clipped, axis=0)]
    lt x1 -> x0, other arithmetic: 10.6 us -> none  [page_states(): owner_rows < row_count]
    reduce_sum x3 -> x0, other arithmetic: 6.54 us -> none  [the longest x1 4.87 us: page_states(): jnp.sum(weights.astype(jnp.float32), axis=4)]
  transfers between devices with their start and end apart: 6 -> 2, of which waited for: 2 -> 2; matrix products, arithmetic and copies ran while one was open for 19% -> 1% of each run, Pallas kernels for 0% -> 0%
where the time goes in v1:
time: 74.5 us; the launch traced here: 73.8 us
  blocking collectives  47.1 us (63%)
  Pallas kernels  19.5 us (26%)
  local copies, waits for them, and re-layouts  3.47 us (5%)
  waiting for transfers between devices  2.29 us (3%)
  other arithmetic  1.46 us (2%)
    all_to_all x3, blocking collectives, exchange(): return lax.all_to_all(x, both, 0, 0, axis_index_groups=members)  47.1 us
    pallas_call x1, Pallas kernels, per_device(): pl.pallas_call(lambda *refs: attend_kernel(chips, *refs), out_shape=jax.S...  8.93 us
    pallas_call x1, Pallas kernels, per_device(): pl.pallas_call(lambda *refs: project_kernel(chips, *refs), out_shape=jax....  5.35 us
    pallas_call x1, Pallas kernels, per_device(): pl.pallas_call(lambda *refs: reduce_kernel(chips, steps, *refs), out_shap...  5.18 us
    ppermute x2, waiting for transfers between devices, per_device(): other = lax.ppermute(own, 'tp', across)  2.29 us
  transfers between devices with their start and end apart: 2, of which 2 were waited for; matrix products, arithmetic and copies ran while one was open for 1% of the time, Pallas kernels for 0%

profile of v1, /device:TPU:0, one launch (start us, length us, event | category | flops | bytes accessed | tf_op | source)
XLA Modules:
  0.0 73.8 jit_solution(16904670054415516208)
XLA Ops:
  0.0 0.7 concatenate.10
  0.7 0.8 %maximum_bitcast_fusion = bf16[16,640]{1,0:T(8,128)(2,1)S(1)} fusion(bf16[1,16,64]{2,1,0:T(8,128)(2,1)} %bitcast.18, bf16[1,16,64]{2,1,0:T(8,128)(2,1)} %bitcast.19, bf16[1,16,512]{2,1,0:T(8,128)(2,1)S(1)} %concatenate.10), kind=kLoop, calls=%fused_computation | loop fusion | flops 61440 | bytes 40960 | tf_op jit(solution)/shard_map/broadcast_in_dim | solution.py:279
  1.5 19.5 %all_to_all.15.refs_4_ = bf16[16,16,640]{2,1,0:T(8,128)(2,1)S(1)} all-to-all(bf16[16,16,640]{2,1,0:T(8,128)(2,1)S(1)} %broadcast_in_dim.8), channel_id=1, replica_groups={{0,2,4,6,8,10,12,14,16,18,20,22,24,26,28,30},{1,3,5,7,9,11,13,15,17,19,..., dimensions={0} | all-to-all | bytes 655360 | tf_op jit(solution)/shard_map/all_to_all | solution.py:254
  21.0 0.0 copy-start
  21.0 0.0 collective-permute-start
  21.0 0.7 pad_add_fusion.refs_0_
  21.7 0.9 %collective-permute-done.refs_5_ = bf16[16,16,640]{2,1,0:T(8,128)(2,1)S(1)} collective-permute-done((bf16[16,16,640]{2,1,0:T(8,128)(2,1)S(1)}, bf16[16,16,640]{2,1,0:T(8,128)(2,1)S(1)}, u32[]{:S(2)}, u32[]{:S(2)}) %collective-permute-start) | collective-permute-done | bytes 327712 | tf_op jit(solution)/shard_map/ppermute | solution.py:281
  22.6 0.0 copy-start.2
  22.6 0.0 copy-done
  22.6 0.7 copy-done.2
  23.4 8.9 %attend.1 = bf16[2,16,48,128]{3,2,1,0:T(8,128)(2,1)} custom-call(s32[3]{0:T(128)} %pad_add_fusion.refs_0_, s32[8]{0:T(128)} %bitcast.20, s32[1,64]{1,0:T(1,128)} %refs_2_.1, s32[1,64]{1,0:T(1,128)} %refs_3_.1, bf16[16,16,640]{2,1,0:T(8,128)(2,1)} %copy-done, bf16[16,16,640]{2,1,0:T(8,128)(2,1)} %copy-done.2, bf16[1024,1024]{1,0:T(8,128)(2,1)} %bitcast.14, ...), custom_call_target="tpu_custom_call" | custom-call | tf_op jit(solution)/shard_map/attend/pallas_call | solution.py:284
  32.3 16.4 %all_to_all.16.refs_1_ = bf16[32,48,128]{2,1,0:T(8,128)(2,1)} all-to-all(bf16[32,48,128]{2,1,0:T(8,128)(2,1)} %bitcast.16), channel_id=1, replica_groups={{0,1,2,3,4,5,6,7,8,9,10,11,12,13,14,15,16,17,18,19,20,21,22,23,24,25,26..., dimensions={0} | all-to-all | bytes 786432 | tf_op jit(solution)/shard_map/all_to_all | solution.py:254
  48.7 5.2 %reduce.1 = bf16[2,8,8,512]{3,2,1,0:T(8,128)(2,1)} custom-call(s32[3]{0:T(128)} %pad_add_fusion.refs_0_, bf16[32,48,128]{2,1,0:T(8,128)(2,1)} %all_to_all.16.refs_1_), custom_call_target="tpu_custom_call" | custom-call | tf_op jit(solution)/shard_map/reduce/pallas_call | solution.py:305
  53.9 11.3 %all_to_all.17.refs_1_ = bf16[16,8,512]{2,1,0:T(8,128)(2,1)S(1)} all-to-all(bf16[16,8,512]{2,1,0:T(8,128)(2,1)} %bitcast.17), channel_id=1, replica_groups={{0,2,4,6,8,10,12,14,16,18,20,22,24,26,28,30},{1,3,5,7,9,11,13,15,17,19,..., dimensions={0} | all-to-all | bytes 262144 | tf_op jit(solution)/shard_map/all_to_all | solution.py:254
  65.1 0.0 copy-start.1
  65.1 0.0 collective-permute-start.1
  65.1 1.3 %collective-permute-done.1.refs_2_ = bf16[16,8,512]{2,1,0:T(8,128)(2,1)S(1)} collective-permute-done((bf16[16,8,512]{2,1,0:T(8,128)(2,1)S(1)}, bf16[16,8,512]{2,1,0:T(8,128)(2,1)S(1)}, u32[]{:S(2)}, u32[]{:S(2)}) %collective-permute-start.1) | collective-permute-done | bytes 131104 | tf_op jit(solution)/shard_map/ppermute | solution.py:313
  66.5 0.0 copy-start.3
  66.5 0.0 copy-done.1
  66.5 0.6 copy-done.3
  67.1 5.3 %project.1 = bf16[16,512]{1,0:T(8,128)(2,1)} custom-call(s32[3]{0:T(128)} %pad_add_fusion.refs_0_, bf16[16,8,512]{2,1,0:T(8,128)(2,1)} %copy-done.1, bf16[16,8,512]{2,1,0:T(8,128)(2,1)} %copy-done.3, bf16[16,512,512]{2,1,0:T(8,128)(2,1)} %bitcast.13), custom_call_target="tpu_custom_call" | custom-call | tf_op jit(solution)/shard_map/project/pallas_call | solution.py:314
  72.5 1.3 %reshape.30 = bf16[1,8,2,512]{3,2,1,0:T(2,128)(2,1)} reshape(bf16[16,512]{1,0:T(8,128)(2,1)} %project.1) | data formatting | bytes 32768 | tf_op jit(solution)/shard_map/reshape | solution.py:321
  (1 shorter events, 0.0 us)
Async XLA Ops:
  21.0 1.6 %copy-start = (bf16[16,16,640]{2,1,0:T(8,128)(2,1)}, bf16[16,16,640]{2,1,0:T(8,128)(2,1)S(1)}, u32[]{:S(2)}) copy-start(bf16[16,16,640]{2,1,0:T(8,128)(2,1)S(1)} %all_to_all.15.refs_4_) | copy-start | bytes 983044
  21.0 1.6 %collective-permute-start = (bf16[16,16,640]{2,1,0:T(8,128)(2,1)S(1)}, bf16[16,16,640]{2,1,0:T(8,128)(2,1)S(1)}, u32[]{:S(2)}, u32[]{:S(2)}) collective-permute-start(bf16[16,16,640]{2,1,0:T(8,128)(2,1)S(1)} %all_to_all.15.refs_4_), channel_id=1, source_target_pairs={{0,1},{1,0},{2,3},{3,2},{4,5},{5,4},{6,7},{7,6},{8,9},{9,8},{10,11... | collective-permute-start | bytes 983048 | tf_op jit(solution)/shard_map/ppermute | solution.py:281
  22.6 0.7 copy-start.2
  65.1 1.4 %copy-start.1 = (bf16[16,8,512]{2,1,0:T(8,128)(2,1)}, bf16[16,8,512]{2,1,0:T(8,128)(2,1)S(1)}, u32[]{:S(2)}) copy-start(bf16[16,8,512]{2,1,0:T(8,128)(2,1)S(1)} %all_to_all.17.refs_1_) | copy-start | bytes 393220
  65.1 1.3 %collective-permute-start.1 = (bf16[16,8,512]{2,1,0:T(8,128)(2,1)S(1)}, bf16[16,8,512]{2,1,0:T(8,128)(2,1)S(1)}, u32[]{:S(2)}, u32[]{:S(2)}) collective-permute-start(bf16[16,8,512]{2,1,0:T(8,128)(2,1)S(1)} %all_to_all.17.refs_1_), channel_id=1, source_target_pairs={{0,1},{1,0},{2,3},{3,2},{4,5},{5,4},{6,7},{7,6},{8,9},{9,8},{10,11... | collective-permute-start | bytes 393224 | tf_op jit(solution)/shard_map/ppermute | solution.py:313
  66.5 0.7 copy-start.3

commit v2 on v1

--- a/solution.py
+++ b/solution.py
@@ -15,6 +15,7 @@
 FLOOR = -1e29
 SCALE = 1.0 / math.sqrt(HD) * math.log2(math.e)
 MOVED_LANE = 64
+TARGET_LANE = 127
 GS = HEADS // KVH
 
 
@@ -26,8 +27,27 @@
     return lax.broadcasted_iota(jnp.int32, shape, axis)
 
 
+def pack_kernel(queries, new_keys, new_values, out):
+    row_steps = out.shape[1]
+    row = jnp.concatenate(
+        [x[...].reshape(row_steps, x.shape[2]) for x in (queries, new_keys, new_values)], axis=1
+    )
+    for i in range(out.shape[0]):
+        out[i] = row
+
+
+def sums_of(aux, local_heads):
+    high = pltpu.roll(aux, HD - local_heads, 1)
+    return high + pltpu.roll(aux, HD - 2 * local_heads, 1)
+
+
+def split(total):
+    high = total.astype(jnp.bfloat16).astype(jnp.float32)
+    return high, total - high
+
+
 def attend_kernel(
-    chips, info, slots, owner, fill, own, other, keys, values, out, bias_own, bias_moved
+    chips, info, slots, owner, fill, own, other, keys, values, keep, send, bias_own, bias_moved
 ):
     row_steps = own.shape[1]
     rows = slots.shape[0]
@@ -120,12 +140,10 @@
             pn.astype(jnp.float32), axis=1, keepdims=True
         )
         acc = dot(p, v, ((1,), (0,))) + dot(pn, in_order(new_v), ((1,), (0,)))
-        high = total.astype(jnp.bfloat16).astype(jnp.float32)
-        low = total - high
+        high, low = split(total)
 
         for side in range(2):
             for kl in range(per_kv):
-                dest = 2 * (g * per_kv + kl) + jnp.where(side == 0, core, 1 - core)
                 t0 = (side * per_kv + kl) * local_heads
                 at_moved = slice(wide + t0 * steps, wide + (t0 + local_heads) * steps)
                 moved_acc = acc[at_moved]
@@ -142,9 +160,9 @@
                         for j in range(local_heads)
                     ]
                     aux = jnp.where(lane == MOVED_LANE, filled(top[at_moved]), 0.0)
-                    aux = jnp.where(lane == MOVED_LANE + 1, filled(high[at_moved]), aux)
-                    aux = jnp.where(lane == MOVED_LANE + 2, filled(low[at_moved]), aux)
-                    aux = jnp.where(lane == MOVED_LANE + 3, target_f, aux)
+                    aux = jnp.where(lane == MOVED_LANE + local_heads, filled(high[at_moved]), aux)
+                    aux = jnp.where(lane == MOVED_LANE + 2 * local_heads, filled(low[at_moved]), aux)
+                    aux = jnp.where(lane == TARGET_LANE, target_f, aux)
                     for j in range(local_heads):
                         rows_at = slice(
                             (t0 + j) * row_steps + h * half_rs,
@@ -154,40 +172,75 @@
                         aux = jnp.where(lane == local_heads + j, high[rows_at], aux)
                         aux = jnp.where(lane == 2 * local_heads + j, low[rows_at], aux)
                     block = jnp.concatenate(parts + [filled(moved_acc), aux], axis=0)
-                    out[h, dest] = block.astype(jnp.bfloat16)
+                    dest = keep if side == 0 else send
+                    dest[h, g * per_kv + kl] = block.astype(jnp.bfloat16)
         return carry
 
     lax.fori_loop(0, KVH, per_head, 0)
 
 
+def merge_kernel(local_heads, first, second, out):
+    half_rs = (first.shape[2]) // (local_heads + 2)
+    span = half_rs * local_heads
+    lane = iota((half_rs, HD), 1)
+    for h in range(first.shape[0]):
+        for k in range(first.shape[1]):
+            a = first[h, k].astype(jnp.float32)
+            b = second[h, k].astype(jnp.float32)
+            aux_a, aux_b = a[span + half_rs :], b[span + half_rs :]
+            top = jnp.maximum(aux_a, aux_b)
+            wa = jnp.exp2(aux_a - top)
+            wb = jnp.exp2(aux_b - top)
+            total = wa * sums_of(aux_a, local_heads) + wb * sums_of(aux_b, local_heads)
+            high, low = split(total)
+            is_top = (lane < local_heads) | (lane >= MOVED_LANE)
+            is_top = is_top & (lane < MOVED_LANE + local_heads) | (lane == TARGET_LANE)
+            high = pltpu.roll(high, local_heads, 1)
+            low = pltpu.roll(low, 2 * local_heads, 1)
+            part = lane % MOVED_LANE // local_heads
+            aux = jnp.where(is_top, top, jnp.where(part == 1, high, low))
+            parts = []
+            for j in range(local_heads + 1):
+                at = j if j < local_heads else MOVED_LANE
+                rows = slice(j * half_rs, (j + 1) * half_rs)
+                parts.append(wa[:, at : at + 1] * a[rows] + wb[:, at : at + 1] * b[rows])
+            out[h, k] = jnp.concatenate(parts + [aux], axis=0).astype(jnp.bfloat16)
+
+
 def reduce_kernel(chips, steps, info, parts, out):
-    sources = 2 * chips
     half_rs = out.shape[2]
     local_heads = out.shape[3] // HD
     half = info[0]
     span = half_rs * local_heads
     row_ids = iota((half_rs, 1), 0)
+    tops, sums, accs = [], [], []
     for g in range(2):
-        blocks = [parts[(1 - g) * sources + t].astype(jnp.float32) for t in range(sources)]
-        aux = [b[span + half_rs :] for b in blocks]
-        column = [a[:, MOVED_LANE : MOVED_LANE + 1] for a in aux]
-        top = column[0]
-        for c in column[1:]:
-            top = jnp.maximum(top, c)
-        moved_sum = jnp.zeros((half_rs, 1), jnp.float32)
-        moved_acc = jnp.zeros((half_rs, HD), jnp.float32)
-        for t in range(sources):
-            w = jnp.exp2(column[t] - top)
-            a = aux[t]
-            moved_sum += w * (
-                a[:, MOVED_LANE + 1 : MOVED_LANE + 2] + a[:, MOVED_LANE + 2 : MOVED_LANE + 3]
-            )
-            moved_acc += w * blocks[t][span : span + half_rs]
-        moved_top = top
-        slot = aux[0][:, MOVED_LANE + 3 : MOVED_LANE + 4]
+        aux = [
+            parts[g * chips + k, span + half_rs :].astype(jnp.float32) for k in range(chips)
+        ]
+        top = aux[0]
+        for a in aux[1:]:
+            top = jnp.maximum(top, a)
+        total = None
+        acc = [None] * (local_heads + 1)
+        for k in range(chips):
+            w = jnp.exp2(aux[k] - top)
+            part = w * sums_of(aux[k], local_heads)
+            total = part if total is None else total + part
+            for j in range(local_heads + 1):
+                at = j if j < local_heads else MOVED_LANE
+                block = parts[g * chips + k, j * half_rs : (j + 1) * half_rs]
+                part = w[:, at : at + 1] * block.astype(jnp.float32)
+                acc[j] = part if acc[j] is None else acc[j] + part
+        tops.append(top)
+        sums.append(total)
+        accs.append(acc)
+    for g in range(2):
+        slot = tops[1 - g][:, TARGET_LANE : TARGET_LANE + 1]
         mine = (half_rs // steps * half + row_ids // steps).astype(jnp.float32) == slot
-        blocks = [parts[g * sources + t].astype(jnp.float32) for t in range(sources)]
-        aux = [b[span + half_rs :] for b in blocks]
+        moved_top = tops[1 - g][:, MOVED_LANE : MOVED_LANE + 1]
+        moved_sum = sums[1 - g][:, MOVED_LANE : MOVED_LANE + 1]
+        moved_acc = accs[1 - g][local_heads]
         done = []
         for j in range(local_heads):
 
@@ -198,23 +251,13 @@
                     y = jnp.where(row_ids % steps == s, z, y)
                 return y
 
-            m_in = jnp.where(mine, placed(moved_top), FLOOR)
-            column = [a[:, j : j + 1] for a in aux]
-            top = m_in
-            for c in column:
-                top = jnp.maximum(top, c)
-            w = jnp.where(mine, jnp.exp2(m_in - top), 0.0)
-            total = w * placed(moved_sum)
-            acc = w * placed(moved_acc)
-            for t in range(sources):
-                w = jnp.exp2(column[t] - top)
-                a = aux[t]
-                total += w * (
-                    a[:, local_heads + j : local_heads + j + 1]
-                    + a[:, 2 * local_heads + j : 2 * local_heads + j + 1]
-                )
-                acc += w * blocks[t][j * half_rs : (j + 1) * half_rs]
-            done.append(acc / total)
+            own_top = tops[g][:, j : j + 1]
+            in_top = jnp.where(mine, placed(moved_top), FLOOR)
+            top = jnp.maximum(own_top, in_top)
+            w_own = jnp.exp2(own_top - top)
+            w_in = jnp.where(mine, jnp.exp2(in_top - top), 0.0)
+            total = w_own * sums[g][:, j : j + 1] + w_in * placed(moved_sum)
+            done.append((w_own * accs[g][j] + w_in * placed(moved_acc)) / total)
         result = jnp.concatenate(done, axis=1).astype(jnp.bfloat16)
         for k in range(chips):
             out[g, k] = result
@@ -229,7 +272,11 @@
             x = jnp.concatenate([source[k], source[chips + k]], axis=0)
             part = dot(x, weight[2 * k + which], ((1,), (0,)))
             acc = part if acc is None else acc + part
-    out[...] = acc.astype(jnp.bfloat16)
+    out[...] = acc.astype(jnp.bfloat16).reshape(out.shape)
+
+
+def limit(mib):
+    return pltpu.CompilerParams(vmem_limit_bytes=mib << 20)
 
 
 SMEM = pl.BlockSpec(memory_space=pltpu.SMEM)
@@ -243,9 +290,6 @@
         [(g + h * apart) * width + 2 * k + c for h in range(2) for k in range(chips)]
         for g in range(apart)
         for c in range(2)
-    ]
-    paired = [
-        [(g + h * apart) * width + t for h in range(2) for t in range(width)] for g in range(apart)
     ]
     across = [(t, t ^ 1) for t in range(width)]
     both = ("group", "tp")
@@ -272,24 +316,33 @@
         tokens = pages * PAGE
         place = lax.axis_index("tp")
         half = lax.axis_index("group") // apart
-        info = jnp.stack([half, place % 2, (place == 0).astype(jnp.int32)]).astype(jnp.int32)
-
-        packed = jnp.concatenate([queries[0], new_keys[0], new_values[0]], axis=2)
-        packed = packed.reshape(1, row_steps, packed.shape[2])
-        sent = jnp.broadcast_to(packed, (2 * chips,) + packed.shape[1:])
+        info = jnp.stack([half, place & 1, (place == 0).astype(jnp.int32)]).astype(jnp.int32)
+
+        sent = pl.pallas_call(
+            pack_kernel,
+            out_shape=jax.ShapeDtypeStruct(
+                (2 * chips, row_steps, features + 2 * new_keys.shape[3]), jnp.bfloat16
+            ),
+            in_specs=[VMEM] * 3,
+            out_specs=VMEM,
+            compiler_params=limit(4),
+            name="pack",
+        )(queries[0], new_keys[0], new_values[0])
         own = exchange(sent, same_core)
         other = lax.ppermute(own, "tp", across)
 
         block_rows = half_rs * local_heads + 2 * half_rs
-        states = pl.pallas_call(
+        state = jax.ShapeDtypeStruct((2, chips, block_rows, HD), jnp.bfloat16)
+        keep, send = pl.pallas_call(
             lambda *refs: attend_kernel(chips, *refs),
-            out_shape=jax.ShapeDtypeStruct((2, width, block_rows, HD), jnp.bfloat16),
+            out_shape=(state, state),
             in_specs=[SMEM, SMEM] + [VMEM] * 6,
-            out_specs=VMEM,
+            out_specs=(VMEM, VMEM),
             scratch_shapes=[
                 pltpu.VMEM((row_steps, tokens), jnp.float32),
                 pltpu.VMEM((GS * steps, tokens), jnp.float32),
             ],
+            compiler_params=limit(16),
             name="attend",
         )(
             info,
@@ -301,24 +354,34 @@
             key_pages.reshape(tokens, key_pages.shape[3]),
             value_pages.reshape(tokens, value_pages.shape[3]),
         )
-        arrived = exchange(states.reshape(2 * width, block_rows, HD), paired)
+        merged = pl.pallas_call(
+            lambda *refs: merge_kernel(local_heads, *refs),
+            out_shape=state,
+            in_specs=[VMEM, VMEM],
+            out_specs=VMEM,
+            compiler_params=limit(4),
+            name="merge",
+        )(keep, lax.ppermute(send, "tp", across))
+        arrived = exchange(merged.reshape(2 * chips, block_rows, HD), same_core)
         finished = pl.pallas_call(
             lambda *refs: reduce_kernel(chips, steps, *refs),
             out_shape=jax.ShapeDtypeStruct((2, chips, half_rs, features), jnp.bfloat16),
             in_specs=[SMEM, VMEM],
             out_specs=VMEM,
+            compiler_params=limit(4),
             name="reduce",
         )(info, arrived)
         own = exchange(finished.reshape(2 * chips, half_rs, features), same_core)
         other = lax.ppermute(own, "tp", across)
         projected = pl.pallas_call(
             lambda *refs: project_kernel(chips, *refs),
-            out_shape=jax.ShapeDtypeStruct((row_steps, out_weight.shape[1]), jnp.bfloat16),
+            out_shape=jax.ShapeDtypeStruct((rows, steps, out_weight.shape[1]), jnp.bfloat16),
             in_specs=[SMEM, VMEM, VMEM, VMEM],
             out_specs=VMEM,
+            compiler_params=limit(16),
             name="project",
         )(info, own, other, out_weight.reshape(width, features, out_weight.shape[1]))
-        return projected.reshape(1, rows, steps, out_weight.shape[1])
+        return projected[None]
 
     return per_device
 

time: 74.5 us -> 68.8 us (0.923)
  Pallas kernels: 19.5 us -> 10.9 us
  local copies, waits for them, and re-layouts: 3.47 us -> 10.6 us
  blocking collectives: 47.1 us -> 42.3 us
  waiting for transfers between devices: 2.29 us -> 4.2 us
  other arithmetic: 1.46 us -> 0.08 us
    unnamed x8 -> x18, local copies, waits for them, and re-layouts: 1.37 us -> 10.6 us
    all_to_all x3, blocking collectives: 47.1 us -> 42.3 us  [exchange(): return lax.all_to_all(x, both, 0, 0, axis_index_groups=members)]
    pallas_call x1, Pallas kernels: 5.18 us -> 1.03 us  [per_device(): pl.pallas_call(lambda *refs: reduce_kernel(chips, steps, *refs), out_shap...]
    pallas_call x1, Pallas kernels: 5.35 us -> 2.35 us  [per_device(): pl.pallas_call(lambda *refs: project_kernel(chips, *refs), out_shape=jax....]
    pallas_call x1 -> x3, Pallas kernels: 8.93 us -> 7.51 us  [the longest x1 6.21 us: per_device(): pl.pallas_call(lambda *refs: attend_kernel(chips, *refs), out_shape=(stat...]
    reshape x1 -> x0, local copies, waits for them, and re-layouts: 1.33 us -> none  [per_device(): return projected.reshape(1, rows, steps, out_weight.shape[1])]
    ppermute x0 -> x1, waiting for transfers between devices: none -> 1.3 us  [per_device(): lax.ppermute(send, 'tp', across)]
    broadcast_in_dim x1 -> x0, other arithmetic: 0.78 us -> none  [per_device(): sent = jnp.broadcast_to(packed, (2 * chips,) + packed.shape[1:])]
  transfers between devices with their start and end apart: 2 -> 3, of which waited for: 2 -> 3; matrix products, arithmetic and copies ran while one was open for 1% -> 0% of each run, Pallas kernels for 0% -> 0%
where the time goes in v2:
time: 68.8 us; the launch traced here: 68.3 us
  blocking collectives  42.3 us (61%)
  Pallas kernels  10.9 us (16%)
  local copies, waits for them, and re-layouts  10.6 us (15%)
  waiting for transfers between devices  4.2 us (6%)
    all_to_all x3, blocking collectives, exchange(): return lax.all_to_all(x, both, 0, 0, axis_index_groups=members)  42.3 us
    unnamed x18, local copies, waits for them, and re-layouts  10.6 us
    pallas_call x1, Pallas kernels, per_device(): pl.pallas_call(lambda *refs: attend_kernel(chips, *refs), out_shape=(stat...  6.21 us
    ppermute x2, waiting for transfers between devices, per_device(): other = lax.ppermute(own, 'tp', across)  2.9 us
    pallas_call x1, Pallas kernels, per_device(): pl.pallas_call(lambda *refs: project_kernel(chips, *refs), out_shape=jax....  2.35 us
  transfers between devices with their start and end apart: 3, of which 3 were waited for; matrix products, arithmetic and copies ran while one was open for 0% of the time, Pallas kernels for 0%

profile of v2, /device:TPU:0, one launch (start us, length us, event | category | flops | bytes accessed | tf_op | source)
XLA Modules:
  0.0 68.3 jit_solution(8086905367772294143)
XLA Ops:
  0.0 0.0 copy-start.3
  0.0 0.7 %copy-done.3 = bf16[1,8,2,512]{3,2,1,0:T(2,128)(2,1)S(1)} copy-done((bf16[1,8,2,512]{3,2,1,0:T(2,128)(2,1)S(1)}, bf16[1,8,2,512]{3,2,1,0:T(2,128)(2,1)}, u32[]{:S(2)}) %copy-start.3) | copy-done | bytes 16408
  0.7 0.0 copy-start.4
  0.7 0.7 %copy-done.4 = bf16[1,8,2,64]{3,2,1,0:T(2,128)(2,1)S(1)} copy-done((bf16[1,8,2,64]{3,2,1,0:T(2,128)(2,1)S(1)}, bf16[1,8,2,64]{3,2,1,0:T(2,128)(2,1)}, u32[]{:S(2)}) %copy-start.4) | copy-done | bytes 2072
  1.4 0.0 copy-start.5
  1.4 0.7 %copy-done.5 = bf16[1,8,2,64]{3,2,1,0:T(2,128)(2,1)S(1)} copy-done((bf16[1,8,2,64]{3,2,1,0:T(2,128)(2,1)S(1)}, bf16[1,8,2,64]{3,2,1,0:T(2,128)(2,1)}, u32[]{:S(2)}) %copy-start.5) | copy-done | bytes 2072
  2.1 0.1 pack.1
  2.2 19.5 %all_to_all.15.refs_4_ = bf16[16,16,640]{2,1,0:T(8,128)(2,1)S(1)} all-to-all(bf16[16,16,640]{2,1,0:T(8,128)(2,1)S(1)} %pack.1), channel_id=1, replica_groups={{0,2,4,6,8,10,12,14,16,18,20,22,24,26,28,30},{1,3,5,7,9,11,13,15,17,19,..., dimensions={0} | all-to-all | bytes 655360 | tf_op jit(solution)/shard_map/all_to_all | solution.py:298
  21.6 0.0 collective-permute-start
  21.6 0.1 pad_add_fusion.refs_0_
  21.7 1.6 %collective-permute-done.refs_5_ = bf16[16,16,640]{2,1,0:T(8,128)(2,1)S(1)} collective-permute-done((bf16[16,16,640]{2,1,0:T(8,128)(2,1)S(1)}, bf16[16,16,640]{2,1,0:T(8,128)(2,1)S(1)}, u32[]{:S(2)}, u32[]{:S(2)}) %collective-permute-start) | collective-permute-done | bytes 327712 | tf_op jit(solution)/shard_map/ppermute | solution.py:332
  23.3 0.0 copy-start.1
  23.3 1.6 %copy-done.1 = bf16[1,64,16,1024]{3,2,1,0:T(8,128)(2,1)S(1)} copy-done((bf16[1,64,16,1024]{3,2,1,0:T(8,128)(2,1)S(1)}, bf16[1,64,16,1024]{3,2,1,0:T(8,128)(2,1)}, u32[]{:S(2)}) %copy-start.1) | copy-done | bytes 2097176
  24.9 0.0 copy-start.2
  24.9 1.6 %copy-done.2 = bf16[1,64,16,1024]{3,2,1,0:T(8,128)(2,1)S(1)} copy-done((bf16[1,64,16,1024]{3,2,1,0:T(8,128)(2,1)S(1)}, bf16[1,64,16,1024]{3,2,1,0:T(8,128)(2,1)}, u32[]{:S(2)}) %copy-start.2) | copy-done | bytes 2097176
  26.5 0.0 copy-start.6
  26.5 0.7 copy-done.6
  27.1 0.0 copy-start.7
  27.1 0.7 copy-done.7
  27.8 0.0 copy-start.8
  27.8 0.7 copy-done.8
  28.4 6.2 %attend.1 = (bf16[2,8,48,128]{3,2,1,0:T(8,128)(2,1)S(1)}, bf16[2,8,48,128]{3,2,1,0:T(8,128)(2,1)S(1)}) custom-call(s32[3]{0:T(128)S(1)} %pad_add_fusion.refs_0_, s32[8]{0:T(128)S(1)} %bitcast.21, s32[1,64]{1,0:T(1,128)S(1)} %copy-done.7, s32[1,64]{1,0:T(1,128)S(1)} %copy-done.8, bf16[16,16,640]{2,1,0:T(8,128)(2,1)S(1)} %all_to_all.15.refs_4_, ...), custom_call_target="tpu_custom_call" | custom-call | tf_op jit(solution)/shard_map/attend/pallas_call | solution.py:336
  34.6 0.2 collective-permute-start.1
  34.8 1.3 %collective-permute-done.1.refs_1_ = bf16[2,8,48,128]{3,2,1,0:T(8,128)(2,1)S(1)} collective-permute-done((bf16[2,8,48,128]{3,2,1,0:T(8,128)(2,1)S(1)}, bf16[2,8,48,128]{3,2,1,0:T(8,128)(2,1)S(1)}, u32[]{:S(2)}, u32[]{:S(2)}) %collective-permute-start.1) | collective-permute-done | bytes 196640 | tf_op jit(solution)/shard_map/ppermute | solution.py:364
  36.1 1.2 %merge.1 = bf16[2,8,48,128]{3,2,1,0:T(8,128)(2,1)S(1)} custom-call(bf16[2,8,48,128]{3,2,1,0:T(8,128)(2,1)S(1)} %get-tuple-element.7.refs_0_, bf16[2,8,48,128]{3,2,1,0:T(8,128)(2,1)S(1)} %collective-permute-done.1.refs_1_), custom_call_target="tpu_custom_call" | custom-call | tf_op jit(solution)/shard_map/merge/pallas_call | solution.py:357
  37.4 11.8 %all_to_all.16.refs_1_ = bf16[16,48,128]{2,1,0:T(8,128)(2,1)S(1)} all-to-all(bf16[16,48,128]{2,1,0:T(8,128)(2,1)S(1)} %bitcast.16), channel_id=1, replica_groups={{0,2,4,6,8,10,12,14,16,18,20,22,24,26,28,30},{1,3,5,7,9,11,13,15,17,19,..., dimensions={0} | all-to-all | bytes 393216 | tf_op jit(solution)/shard_map/all_to_all | solution.py:298
  49.1 1.0 %reduce.1 = bf16[2,8,8,512]{3,2,1,0:T(8,128)(2,1)S(1)} custom-call(s32[3]{0:T(128)S(1)} %pad_add_fusion.refs_0_, bf16[16,48,128]{2,1,0:T(8,128)(2,1)S(1)} %all_to_all.16.refs_1_), custom_call_target="tpu_custom_call" | custom-call | tf_op jit(solution)/shard_map/reduce/pallas_call | solution.py:366
  50.2 11.1 %all_to_all.17.refs_1_ = bf16[16,8,512]{2,1,0:T(8,128)(2,1)S(1)} all-to-all(bf16[16,8,512]{2,1,0:T(8,128)(2,1)S(1)} %bitcast.17), channel_id=1, replica_groups={{0,2,4,6,8,10,12,14,16,18,20,22,24,26,28,30},{1,3,5,7,9,11,13,15,17,19,..., dimensions={0} | all-to-all | bytes 262144 | tf_op jit(solution)/shard_map/all_to_all | solution.py:298
  61.3 0.0 collective-permute-start.2
  61.3 1.3 %collective-permute-done.2.refs_2_ = bf16[16,8,512]{2,1,0:T(8,128)(2,1)S(1)} collective-permute-done((bf16[16,8,512]{2,1,0:T(8,128)(2,1)S(1)}, bf16[16,8,512]{2,1,0:T(8,128)(2,1)S(1)}, u32[]{:S(2)}, u32[]{:S(2)}) %collective-permute-start.2) | collective-permute-done | bytes 131104 | tf_op jit(solution)/shard_map/ppermute | solution.py:375
  62.6 0.0 copy-start
  62.6 3.4 %copy-done = bf16[8192,512]{1,0:T(8,128)(2,1)S(1)} copy-done((bf16[8192,512]{1,0:T(8,128)(2,1)S(1)}, bf16[8192,512]{1,0:T(8,128)(2,1)}, u32[]{:S(2)}) %copy-start) | copy-done | bytes 8388632
  66.0 2.3 %project.1 = bf16[8,2,512]{2,1,0:T(2,128)(2,1)} custom-call(s32[3]{0:T(128)S(1)} %pad_add_fusion.refs_0_, bf16[16,8,512]{2,1,0:T(8,128)(2,1)S(1)} %all_to_all.17.refs_1_, bf16[16,8,512]{2,1,0:T(8,128)(2,1)S(1)} %collective-permute-done.2.refs_2_, bf16[16,512,512]{2,1,0:T(8,128)(2,1)S(1)} %bitcast.13), custom_call_target="tpu_custom_call" | custom-call | tf_op jit(solution)/shard_map/project/pallas_call | solution.py:376
Async XLA Ops:
  0.0 0.7 %copy-start.3 = (bf16[1,8,2,512]{3,2,1,0:T(2,128)(2,1)S(1)}, bf16[1,8,2,512]{3,2,1,0:T(2,128)(2,1)}, u32[]{:S(2)}) copy-start(bf16[1,8,2,512]{3,2,1,0:T(2,128)(2,1)} %param.9) | copy-start | bytes 49156
  0.7 0.7 %copy-start.4 = (bf16[1,8,2,64]{3,2,1,0:T(2,128)(2,1)S(1)}, bf16[1,8,2,64]{3,2,1,0:T(2,128)(2,1)}, u32[]{:S(2)}) copy-start(bf16[1,8,2,64]{3,2,1,0:T(2,128)(2,1)} %param.10) | copy-start | bytes 6148
  1.4 0.7 %copy-start.5 = (bf16[1,8,2,64]{3,2,1,0:T(2,128)(2,1)S(1)}, bf16[1,8,2,64]{3,2,1,0:T(2,128)(2,1)}, u32[]{:S(2)}) copy-start(bf16[1,8,2,64]{3,2,1,0:T(2,128)(2,1)} %param.11) | copy-start | bytes 6148
  21.6 1.6 %collective-permute-start = (bf16[16,16,640]{2,1,0:T(8,128)(2,1)S(1)}, bf16[16,16,640]{2,1,0:T(8,128)(2,1)S(1)}, u32[]{:S(2)}, u32[]{:S(2)}) collective-permute-start(bf16[16,16,640]{2,1,0:T(8,128)(2,1)S(1)} %all_to_all.15.refs_4_), channel_id=1, source_target_pairs={{0,1},{1,0},{2,3},{3,2},{4,5},{5,4},{6,7},{7,6},{8,9},{9,8},{10,11... | collective-permute-start | bytes 983048 | tf_op jit(solution)/shard_map/ppermute | solution.py:332
  23.3 1.6 %copy-start.1 = (bf16[1,64,16,1024]{3,2,1,0:T(8,128)(2,1)S(1)}, bf16[1,64,16,1024]{3,2,1,0:T(8,128)(2,1)}, u32[]{:S(2)}) copy-start(bf16[1,64,16,1024]{3,2,1,0:T(8,128)(2,1)} %param.12) | copy-start | bytes 6291460
  24.9 1.6 %copy-start.2 = (bf16[1,64,16,1024]{3,2,1,0:T(8,128)(2,1)S(1)}, bf16[1,64,16,1024]{3,2,1,0:T(8,128)(2,1)}, u32[]{:S(2)}) copy-start(bf16[1,64,16,1024]{3,2,1,0:T(8,128)(2,1)} %param.13) | copy-start | bytes 6291460
  26.5 0.7 copy-start.6
  27.1 0.7 copy-start.7
  27.8 0.7 copy-start.8
  34.6 1.5 %collective-permute-start.1 = (bf16[2,8,48,128]{3,2,1,0:T(8,128)(2,1)S(1)}, bf16[2,8,48,128]{3,2,1,0:T(8,128)(2,1)S(1)}, u32[]{:S(2)}, u32[]{:S(2)}) collective-permute-start(bf16[2,8,48,128]{3,2,1,0:T(8,128)(2,1)S(1)} %get-tuple-element.8), channel_id=1, source_target_pairs={{0,1},{1,0},{2,3},{3,2},{4,5},{5,4},{6,7},{7,6},{8,9},{9,8},{10,11... | collective-permute-start | bytes 589832 | tf_op jit(solution)/shard_map/ppermute | solution.py:364
  61.3 1.3 %collective-permute-start.2 = (bf16[16,8,512]{2,1,0:T(8,128)(2,1)S(1)}, bf16[16,8,512]{2,1,0:T(8,128)(2,1)S(1)}, u32[]{:S(2)}, u32[]{:S(2)}) collective-permute-start(bf16[16,8,512]{2,1,0:T(8,128)(2,1)S(1)} %all_to_all.17.refs_1_), channel_id=1, source_target_pairs={{0,1},{1,0},{2,3},{3,2},{4,5},{5,4},{6,7},{7,6},{8,9},{9,8},{10,11... | collective-permute-start | bytes 393224 | tf_op jit(solution)/shard_map/ppermute | solution.py:375
  62.6 3.4 %copy-start = (bf16[8192,512]{1,0:T(8,128)(2,1)S(1)}, bf16[8192,512]{1,0:T(8,128)(2,1)}, u32[]{:S(2)}) copy-start(bf16[8192,512]{1,0:T(8,128)(2,1)} %param.17) | copy-start | bytes 25165828

commit v3 on v2

--- a/solution.py
+++ b/solution.py
@@ -17,6 +17,7 @@
 MOVED_LANE = 64
 TARGET_LANE = 127
 GS = HEADS // KVH
+UNROLL = 1
 
 
 def dot(a, b, contract):
@@ -27,11 +28,18 @@
     return lax.broadcasted_iota(jnp.int32, shape, axis)
 
 
-def pack_kernel(queries, new_keys, new_values, out):
+def pack_kernel(queries, new_keys, new_values, out, q_buf, k_buf, v_buf, sems):
     row_steps = out.shape[1]
-    row = jnp.concatenate(
-        [x[...].reshape(row_steps, x.shape[2]) for x in (queries, new_keys, new_values)], axis=1
-    )
+    buffers = (q_buf, k_buf, v_buf)
+    copies = [
+        pltpu.make_async_copy(x, b, sems.at[i])
+        for i, (x, b) in enumerate(zip((queries, new_keys, new_values), buffers))
+    ]
+    for c in copies:
+        c.start()
+    for c in copies:
+        c.wait()
+    row = jnp.concatenate([b[...].reshape(row_steps, b.shape[2]) for b in buffers], axis=1)
     for i in range(out.shape[0]):
         out[i] = row
 
@@ -47,26 +55,72 @@
 
 
 def attend_kernel(
-    chips, info, slots, owner, fill, own, other, keys, values, keep, send, bias_own, bias_moved
+    chips,
+    info,
+    slots_hbm,
+    owner_hbm,
+    fill_hbm,
+    own,
+    other,
+    keys_hbm,
+    values_hbm,
+    weight_hbm,
+    keep,
+    send,
+    weight,
+    bias_own,
+    bias_moved,
+    slots,
+    owner,
+    fill,
+    keys,
+    values,
+    small_sems,
+    kv_sems,
+    weight_sems,
 ):
     row_steps = own.shape[1]
-    rows = slots.shape[0]
+    rows = slots.shape[1]
     steps = row_steps // rows
     features = HEADS // (2 * chips) * HD
     local_heads = features // HD
     kv_part = (own.shape[2] - features) // 2
     per_kv = chips // KVH
-    tokens = keys.shape[0]
+    tokens = keys.shape[1]
     half_rs = row_steps // 2
+    pieces = weight.shape[0] // KVH
+
+    def kv_copy(g, which):
+        at = pl.ds(pl.multiple_of(g * HD, HD), HD)
+        source, target = ((keys_hbm, keys), (values_hbm, values))[which]
+        return pltpu.make_async_copy(source.at[:, at], target.at[g], kv_sems.at[which, g])
+
+    def weight_copy(g):
+        at = pl.ds(g * pieces, pieces)
+        return pltpu.make_async_copy(weight_hbm.at[at], weight.at[at], weight_sems.at[g])
+
+    small = [
+        pltpu.make_async_copy(source, target, small_sems.at[i])
+        for i, (source, target) in enumerate(
+            ((slots_hbm, slots), (owner_hbm, owner), (fill_hbm, fill))
+        )
+    ]
+    for c in small:
+        c.start()
+    for g in range(KVH):
+        kv_copy(g, 0).start()
+        kv_copy(g, 1).start()
+    for c in small:
+        c.wait()
     half = info[0]
     core = info[1]
     first = info[2]
     mover = jnp.int32(0)
     target = jnp.int32(0)
     for r in range(rows):
-        leaves = slots[r] < rows
+        leaves = slots[0, r] < rows
         mover = jnp.where(leaves, r, mover)
-        target = jnp.where(leaves, slots[r], target)
+        target = jnp.where(leaves, slots[0, r], target)
 
     pages = owner.shape[1]
     spread = (iota((pages, tokens), 1) // PAGE == iota((pages, tokens), 0)).astype(jnp.bfloat16)
@@ -96,6 +150,9 @@
     target_f = target.astype(jnp.float32)
 
     def per_head(g, carry):
+        weight_copy(g).start()
+        kv_copy(g, 0).wait()
+        kv_copy(g, 1).wait()
         tiles, partner_tiles, new_k, new_v = [], [], [], []
         for source in (own, other):
             for kl in range(per_kv):
@@ -119,9 +176,8 @@
 
         moved_q = dot(pick, jnp.concatenate(partner_tiles, axis=0), ((1,), (0,)))
         q = jnp.concatenate(tiles + [moved_q.astype(jnp.bfloat16)], axis=0)
-        at = pl.ds(pl.multiple_of(g * HD, HD), HD)
-        k = keys[:, at]
-        v = values[:, at]
+        k = keys[g]
+        v = values[g]
         scores = dot(q, k, ((1,), (1,))) * SCALE
         bias = jnp.concatenate([bias_own[...]] * GS + [bias_moved[...]], axis=0)
         scores = scores + bias
@@ -176,7 +232,9 @@
                     dest[h, g * per_kv + kl] = block.astype(jnp.bfloat16)
         return carry
 
-    lax.fori_loop(0, KVH, per_head, 0)
+    lax.fori_loop(0, KVH, per_head, 0, unroll=UNROLL)
+    for g in range(KVH):
+        weight_copy(g).wait()
 
 
 def merge_kernel(local_heads, first, second, out):
@@ -275,12 +333,17 @@
     out[...] = acc.astype(jnp.bfloat16).reshape(out.shape)
 
 
+def in_hbm(x):
+    return pltpu.with_memory_space_constraint(x, pltpu.HBM)
+
+
 def limit(mib):
     return pltpu.CompilerParams(vmem_limit_bytes=mib << 20)
 
 
 SMEM = pl.BlockSpec(memory_space=pltpu.SMEM)
 VMEM = pl.BlockSpec(memory_space=pltpu.VMEM)
+HBM = pl.BlockSpec(memory_space=pltpu.HBM)
 
 
 def per_device_of(groups, width):
@@ -323,36 +386,54 @@
             out_shape=jax.ShapeDtypeStruct(
                 (2 * chips, row_steps, features + 2 * new_keys.shape[3]), jnp.bfloat16
             ),
-            in_specs=[VMEM] * 3,
+            in_specs=[HBM] * 3,
             out_specs=VMEM,
+            scratch_shapes=[
+                pltpu.VMEM(x.shape[1:], x.dtype) for x in (queries, new_keys, new_values)
+            ]
+            + [pltpu.SemaphoreType.DMA((3,))],
             compiler_params=limit(4),
             name="pack",
-        )(queries[0], new_keys[0], new_values[0])
+        )(*(in_hbm(x[0]) for x in (queries, new_keys, new_values)))
         own = exchange(sent, same_core)
         other = lax.ppermute(own, "tp", across)
 
         block_rows = half_rs * local_heads + 2 * half_rs
         state = jax.ShapeDtypeStruct((2, chips, block_rows, HD), jnp.bfloat16)
-        keep, send = pl.pallas_call(
+        weight_by_device = out_weight.reshape(width, features, out_weight.shape[1])
+        keep, send, weight = pl.pallas_call(
             lambda *refs: attend_kernel(chips, *refs),
-            out_shape=(state, state),
-            in_specs=[SMEM, SMEM] + [VMEM] * 6,
-            out_specs=(VMEM, VMEM),
+            out_shape=(
+                state,
+                state,
+                jax.ShapeDtypeStruct(weight_by_device.shape, weight_by_device.dtype),
+            ),
+            in_specs=[SMEM] + [HBM] * 3 + [VMEM] * 2 + [HBM] * 3,
+            out_specs=(VMEM, VMEM, VMEM),
             scratch_shapes=[
                 pltpu.VMEM((row_steps, tokens), jnp.float32),
                 pltpu.VMEM((GS * steps, tokens), jnp.float32),
+                pltpu.SMEM(target_slot.shape, jnp.int32),
+                pltpu.VMEM(page_owner.shape, jnp.int32),
+                pltpu.VMEM(page_fill.shape, jnp.int32),
+                pltpu.VMEM((KVH, tokens, HD), jnp.bfloat16),
+                pltpu.VMEM((KVH, tokens, HD), jnp.bfloat16),
+                pltpu.SemaphoreType.DMA((3,)),
+                pltpu.SemaphoreType.DMA((2, KVH)),
+                pltpu.SemaphoreType.DMA((KVH,)),
             ],
-            compiler_params=limit(16),
+            compiler_params=limit(28),
             name="attend",
         )(
             info,
-            target_slot[0],
-            page_owner,
-            page_fill,
+            in_hbm(target_slot),
+            in_hbm(page_owner),
+            in_hbm(page_fill),
             own,
             other,
-            key_pages.reshape(tokens, key_pages.shape[3]),
-            value_pages.reshape(tokens, value_pages.shape[3]),
+            in_hbm(key_pages.reshape(tokens, key_pages.shape[3])),
+            in_hbm(value_pages.reshape(tokens, value_pages.shape[3])),
+            in_hbm(weight_by_device),
         )
         merged = pl.pallas_call(
             lambda *refs: merge_kernel(local_heads, *refs),
@@ -380,7 +461,7 @@
             out_specs=VMEM,
             compiler_params=limit(16),
             name="project",
-        )(info, own, other, out_weight.reshape(width, features, out_weight.shape[1]))
+        )(info, own, other, weight)
         return projected[None]
 
     return per_device

time: 68.8 us -> 61.6 us (0.90)
  local copies, waits for them, and re-layouts: 10.6 us -> 0 us
  Pallas kernels: 10.9 us -> 14.4 us
    unnamed x18 -> x0, local copies, waits for them, and re-layouts: 10.6 us -> none
    pallas_call x1, Pallas kernels: 6.21 us -> 9.01 us  [per_device(): pl.pallas_call(lambda *refs: attend_kernel(chips, *refs), out_shape=(stat...]
    pallas_call x1, Pallas kernels: 0.09 us -> 0.83 us  [per_device(): pl.pallas_call(pack_kernel, out_shape=jax.ShapeDtypeStruct((2 * chips, ro...]
where the time goes in v3:
time: 61.6 us; the launch traced here: 61.3 us
  blocking collectives  42.3 us (69%)
  Pallas kernels  14.4 us (23%)
  waiting for transfers between devices  4.2 us (7%)
    all_to_all x3, blocking collectives, exchange(): return lax.all_to_all(x, both, 0, 0, axis_index_groups=members)  42.3 us
    pallas_call x1, Pallas kernels, per_device(): pl.pallas_call(lambda *refs: attend_kernel(chips, *refs), out_shape=(stat...  9.01 us
    ppermute x2, waiting for transfers between devices, per_device(): other = lax.ppermute(own, 'tp', across)  2.9 us
    pallas_call x1, Pallas kernels, per_device(): pl.pallas_call(lambda *refs: project_kernel(chips, *refs), out_shape=jax....  2.35 us
    ppermute x1, waiting for transfers between devices, per_device(): lax.ppermute(send, 'tp', across)  1.3 us
  transfers between devices with their start and end apart: 3, of which 3 were waited for; matrix products, arithmetic and copies ran while one was open for 0% of the time, Pallas kernels for 0%

profile of v3, /device:TPU:0, one launch (start us, length us, event | category | flops | bytes accessed | tf_op | source)
XLA Modules:
  0.0 61.3 jit_solution(232798016442697960)
XLA Ops:
  0.0 0.8 %pack.1 = bf16[16,16,640]{2,1,0:T(8,128)(2,1)S(1)} custom-call(bf16[8,2,512]{2,1,0:T(2,128)(2,1)} %bitcast.17, bf16[8,2,64]{2,1,0:T(2,128)(2,1)} %bitcast.18, bf16[8,2,64]{2,1,0:T(2,128)(2,1)} %bitcast.19), custom_call_target="tpu_custom_call" | custom-call | tf_op jit(solution)/shard_map/pack/pallas_call | solution.py:384
  0.8 19.5 %all_to_all.15.refs_4_ = bf16[16,16,640]{2,1,0:T(8,128)(2,1)S(1)} all-to-all(bf16[16,16,640]{2,1,0:T(8,128)(2,1)S(1)} %pack.1), channel_id=1, replica_groups={{0,2,4,6,8,10,12,14,16,18,20,22,24,26,28,30},{1,3,5,7,9,11,13,15,17,19,..., dimensions={0} | all-to-all | bytes 655360 | tf_op jit(solution)/shard_map/all_to_all | solution.py:361
  20.3 0.0 collective-permute-start
  20.3 0.1 pad_add_fusion.refs_0_
  20.4 1.6 %collective-permute-done.refs_5_ = bf16[16,16,640]{2,1,0:T(8,128)(2,1)S(1)} collective-permute-done((bf16[16,16,640]{2,1,0:T(8,128)(2,1)S(1)}, bf16[16,16,640]{2,1,0:T(8,128)(2,1)S(1)}, u32[]{:S(2)}, u32[]{:S(2)}) %collective-permute-start) | collective-permute-done | bytes 327712 | tf_op jit(solution)/shard_map/ppermute | solution.py:399
  21.9 9.0 %attend.1 = (bf16[2,8,48,128]{3,2,1,0:T(8,128)(2,1)S(1)}, bf16[2,8,48,128]{3,2,1,0:T(8,128)(2,1)S(1)}, bf16[16,512,512]{2,1,0:T(8,128)(2,1)S(1)}) custom-call(s32[3]{0:T(128)S(1)} %pad_add_fusion.refs_0_, s32[1,8]{1,0:T(1,128)} %refs_1_.1, s32[1,64]{1,0:T(1,128)} %refs_2_.1, s32[1,64]{1,0:T(1,128)} %refs_3_.1, bf16[16,16,640]{2,1,0:T(8,128)(2,1)S(1)} %all_to_all.15.refs_4_, ...), custom_call_target="tpu_custom_call" | custom-call | tf_op jit(solution)/shard_map/attend/pallas_call | solution.py:404
  30.9 0.2 collective-permute-start.1
  31.2 1.3 %collective-permute-done.1.refs_1_ = bf16[2,8,48,128]{3,2,1,0:T(8,128)(2,1)S(1)} collective-permute-done((bf16[2,8,48,128]{3,2,1,0:T(8,128)(2,1)S(1)}, bf16[2,8,48,128]{3,2,1,0:T(8,128)(2,1)S(1)}, u32[]{:S(2)}, u32[]{:S(2)}) %collective-permute-start.1) | collective-permute-done | bytes 196640 | tf_op jit(solution)/shard_map/ppermute | solution.py:445
  32.5 1.2 %merge.1 = bf16[2,8,48,128]{3,2,1,0:T(8,128)(2,1)S(1)} custom-call(bf16[2,8,48,128]{3,2,1,0:T(8,128)(2,1)S(1)} %get-tuple-element.8.refs_0_, bf16[2,8,48,128]{3,2,1,0:T(8,128)(2,1)S(1)} %collective-permute-done.1.refs_1_), custom_call_target="tpu_custom_call" | custom-call | tf_op jit(solution)/shard_map/merge/pallas_call | solution.py:438
  33.7 11.8 %all_to_all.16.refs_1_ = bf16[16,48,128]{2,1,0:T(8,128)(2,1)S(1)} all-to-all(bf16[16,48,128]{2,1,0:T(8,128)(2,1)S(1)} %bitcast.12), channel_id=1, replica_groups={{0,2,4,6,8,10,12,14,16,18,20,22,24,26,28,30},{1,3,5,7,9,11,13,15,17,19,..., dimensions={0} | all-to-all | bytes 393216 | tf_op jit(solution)/shard_map/all_to_all | solution.py:361
  45.4 1.0 %reduce.1 = bf16[2,8,8,512]{3,2,1,0:T(8,128)(2,1)S(1)} custom-call(s32[3]{0:T(128)S(1)} %pad_add_fusion.refs_0_, bf16[16,48,128]{2,1,0:T(8,128)(2,1)S(1)} %all_to_all.16.refs_1_), custom_call_target="tpu_custom_call" | custom-call | tf_op jit(solution)/shard_map/reduce/pallas_call | solution.py:447
  46.5 11.1 %all_to_all.17.refs_1_ = bf16[16,8,512]{2,1,0:T(8,128)(2,1)S(1)} all-to-all(bf16[16,8,512]{2,1,0:T(8,128)(2,1)S(1)} %bitcast.13), channel_id=1, replica_groups={{0,2,4,6,8,10,12,14,16,18,20,22,24,26,28,30},{1,3,5,7,9,11,13,15,17,19,..., dimensions={0} | all-to-all | bytes 262144 | tf_op jit(solution)/shard_map/all_to_all | solution.py:361
  57.6 0.0 collective-permute-start.2
  57.6 1.3 %collective-permute-done.2.refs_2_ = bf16[16,8,512]{2,1,0:T(8,128)(2,1)S(1)} collective-permute-done((bf16[16,8,512]{2,1,0:T(8,128)(2,1)S(1)}, bf16[16,8,512]{2,1,0:T(8,128)(2,1)S(1)}, u32[]{:S(2)}, u32[]{:S(2)}) %collective-permute-start.2) | collective-permute-done | bytes 131104 | tf_op jit(solution)/shard_map/ppermute | solution.py:456
  58.9 2.3 %project.1 = bf16[8,2,512]{2,1,0:T(2,128)(2,1)} custom-call(s32[3]{0:T(128)S(1)} %pad_add_fusion.refs_0_, bf16[16,8,512]{2,1,0:T(8,128)(2,1)S(1)} %all_to_all.17.refs_1_, bf16[16,8,512]{2,1,0:T(8,128)(2,1)S(1)} %collective-permute-done.2.refs_2_, bf16[16,512,512]{2,1,0:T(8,128)(2,1)S(1)} %get-tuple-element.10.refs_3_), custom_call_target="tpu_custom_call" | custom-call | tf_op jit(solution)/shard_map/project/pallas_call | solution.py:457
Async XLA Ops:
  20.3 1.6 %collective-permute-start = (bf16[16,16,640]{2,1,0:T(8,128)(2,1)S(1)}, bf16[16,16,640]{2,1,0:T(8,128)(2,1)S(1)}, u32[]{:S(2)}, u32[]{:S(2)}) collective-permute-start(bf16[16,16,640]{2,1,0:T(8,128)(2,1)S(1)} %all_to_all.15.refs_4_), channel_id=1, source_target_pairs={{0,1},{1,0},{2,3},{3,2},{4,5},{5,4},{6,7},{7,6},{8,9},{9,8},{10,11... | collective-permute-start | bytes 983048 | tf_op jit(solution)/shard_map/ppermute | solution.py:399
  30.9 1.5 %collective-permute-start.1 = (bf16[2,8,48,128]{3,2,1,0:T(8,128)(2,1)S(1)}, bf16[2,8,48,128]{3,2,1,0:T(8,128)(2,1)S(1)}, u32[]{:S(2)}, u32[]{:S(2)}) collective-permute-start(bf16[2,8,48,128]{3,2,1,0:T(8,128)(2,1)S(1)} %get-tuple-element.9), channel_id=1, source_target_pairs={{0,1},{1,0},{2,3},{3,2},{4,5},{5,4},{6,7},{7,6},{8,9},{9,8},{10,11... | collective-permute-start | bytes 589832 | tf_op jit(solution)/shard_map/ppermute | solution.py:445
  57.6 1.3 %collective-permute-start.2 = (bf16[16,8,512]{2,1,0:T(8,128)(2,1)S(1)}, bf16[16,8,512]{2,1,0:T(8,128)(2,1)S(1)}, u32[]{:S(2)}, u32[]{:S(2)}) collective-permute-start(bf16[16,8,512]{2,1,0:T(8,128)(2,1)S(1)} %all_to_all.17.refs_1_), channel_id=1, source_target_pairs={{0,1},{1,0},{2,3},{3,2},{4,5},{5,4},{6,7},{7,6},{8,9},{9,8},{10,11... | collective-permute-start | bytes 393224 | tf_op jit(solution)/shard_map/ppermute | solution.py:456

commit v4 on v2

--- a/solution.py
+++ b/solution.py
@@ -17,6 +17,7 @@
 MOVED_LANE = 64
 TARGET_LANE = 127
 GS = HEADS // KVH
+UNROLL = 2
 
 
 def dot(a, b, contract):
@@ -27,11 +28,18 @@
     return lax.broadcasted_iota(jnp.int32, shape, axis)
 
 
-def pack_kernel(queries, new_keys, new_values, out):
+def pack_kernel(queries, new_keys, new_values, out, q_buf, k_buf, v_buf, sems):
     row_steps = out.shape[1]
-    row = jnp.concatenate(
-        [x[...].reshape(row_steps, x.shape[2]) for x in (queries, new_keys, new_values)], axis=1
-    )
+    buffers = (q_buf, k_buf, v_buf)
+    copies = [
+        pltpu.make_async_copy(x, b, sems.at[i])
+        for i, (x, b) in enumerate(zip((queries, new_keys, new_values), buffers))
+    ]
+    for c in copies:
+        c.start()
+    for c in copies:
+        c.wait()
+    row = jnp.concatenate([b[...].reshape(row_steps, b.shape[2]) for b in buffers], axis=1)
     for i in range(out.shape[0]):
         out[i] = row
 
@@ -46,28 +54,48 @@
     return high, total - high
 
 
-def attend_kernel(
-    chips, info, slots, owner, fill, own, other, keys, values, keep, send, bias_own, bias_moved
-):
-    row_steps = own.shape[1]
-    rows = slots.shape[0]
-    steps = row_steps // rows
-    features = HEADS // (2 * chips) * HD
-    local_heads = features // HD
-    kv_part = (own.shape[2] - features) // 2
-    per_kv = chips // KVH
-    tokens = keys.shape[0]
-    half_rs = row_steps // 2
-    half = info[0]
-    core = info[1]
-    first = info[2]
+def mover_of(slots):
+    rows = slots.shape[1]
     mover = jnp.int32(0)
     target = jnp.int32(0)
     for r in range(rows):
-        leaves = slots[r] < rows
+        leaves = slots[0, r] < rows
         mover = jnp.where(leaves, r, mover)
-        target = jnp.where(leaves, slots[r], target)
-
+        target = jnp.where(leaves, slots[0, r], target)
+    return mover, target
+
+
+def prepare_kernel(
+    steps,
+    slots_hbm,
+    owner_hbm,
+    fill_hbm,
+    keys_hbm,
+    values_hbm,
+    after,
+    keys,
+    values,
+    bias_own,
+    bias_moved,
+    slots,
+    owner,
+    fill,
+    sems,
+):
+    del after
+    rows = slots.shape[1]
+    row_steps, tokens = bias_own.shape
+    sources = (slots_hbm, owner_hbm, fill_hbm, keys_hbm, values_hbm)
+    targets = (slots, owner, fill, keys, values)
+    copies = [
+        pltpu.make_async_copy(source, target, sems.at[i])
+        for i, (source, target) in enumerate(zip(sources, targets))
+    ]
+    for c in copies:
+        c.start()
+    for c in copies[:3]:
+        c.wait()
+    mover, _ = mover_of(slots)
     pages = owner.shape[1]
     spread = (iota((pages, tokens), 1) // PAGE == iota((pages, tokens), 0)).astype(jnp.bfloat16)
     table = jnp.concatenate([owner[...], fill[...]], axis=0).astype(jnp.float32)
@@ -80,6 +108,43 @@
     stay_row = jnp.where(token_row == mover, rows, token_row)
     bias_own[...] = jnp.where(iota((row_steps, tokens), 0) // steps == stay_row, 0.0, NEG)
     bias_moved[...] = jnp.broadcast_to(jnp.where(token_row == mover, 0.0, NEG), bias_moved.shape)
+    for c in copies[3:]:
+        c.wait()
+
+
+def attend_kernel(
+    chips,
+    info,
+    slots,
+    own,
+    other,
+    keys,
+    values,
+    bias_own,
+    bias_moved,
+    weight_hbm,
+    keep,
+    send,
+    weight,
+    weight_sems,
+):
+    row_steps = own.shape[1]
+    steps = row_steps // slots.shape[1]
+    features = HEADS // (2 * chips) * HD
+    local_heads = features // HD
+    kv_part = (own.shape[2] - features) // 2
+    per_kv = chips // KVH
+    half_rs = row_steps // 2
+    half = info[0]
+    core = info[1]
+    first = info[2]
+    _, target = mover_of(slots)
+    copies = [
+        pltpu.make_async_copy(weight_hbm.at[i], weight.at[i], weight_sems.at[i])
+        for i in range(weight.shape[0])
+    ]
+    for c in copies:
+        c.start()
 
     rs_ids = iota((row_steps, row_steps), 0)
     new_ids = iota((row_steps, row_steps), 1)
@@ -176,7 +241,9 @@
                     dest[h, g * per_kv + kl] = block.astype(jnp.bfloat16)
         return carry
 
-    lax.fori_loop(0, KVH, per_head, 0)
+    lax.fori_loop(0, KVH, per_head, 0, unroll=UNROLL)
+    for c in copies:
+        c.wait()
 
 
 def merge_kernel(local_heads, first, second, out):
@@ -263,16 +330,26 @@
             out[g, k] = result
 
 
-def project_kernel(chips, info, own, other, weight, out):
-    core = info[1]
+def project(chips, which, source, weight):
     acc = None
-    for side, source in enumerate((own, other)):
-        which = core if side == 0 else 1 - core
-        for k in range(chips):
-            x = jnp.concatenate([source[k], source[chips + k]], axis=0)
-            part = dot(x, weight[2 * k + which], ((1,), (0,)))
-            acc = part if acc is None else acc + part
-    out[...] = acc.astype(jnp.bfloat16).reshape(out.shape)
+    for k in range(chips):
+        x = jnp.concatenate([source[k], source[chips + k]], axis=0)
+        part = dot(x, weight[2 * k + which], ((1,), (0,)))
+        acc = part if acc is None else acc + part
+    return acc
+
+
+def project_own_kernel(chips, info, own, weight, out):
+    out[...] = project(chips, info[1], own, weight)
+
+
+def project_other_kernel(chips, info, partial, other, weight, out):
+    total = partial[...] + project(chips, 1 - info[1], other, weight)
+    out[...] = total.astype(jnp.bfloat16).reshape(out.shape)
+
+
+def in_hbm(x):
+    return pltpu.with_memory_space_constraint(x, pltpu.HBM)
 
 
 def limit(mib):
@@ -281,6 +358,8 @@
 
 SMEM = pl.BlockSpec(memory_space=pltpu.SMEM)
 VMEM = pl.BlockSpec(memory_space=pltpu.VMEM)
+HBM = pl.BlockSpec(memory_space=pltpu.HBM)
+ANY = pl.BlockSpec(memory_space=pl.ANY)
 
 
 def per_device_of(groups, width):
@@ -323,36 +402,69 @@
             out_shape=jax.ShapeDtypeStruct(
                 (2 * chips, row_steps, features + 2 * new_keys.shape[3]), jnp.bfloat16
             ),
-            in_specs=[VMEM] * 3,
+            in_specs=[HBM] * 3,
             out_specs=VMEM,
+            scratch_shapes=[
+                pltpu.VMEM(x.shape[1:], x.dtype) for x in (queries, new_keys, new_values)
+            ]
+            + [pltpu.SemaphoreType.DMA((3,))],
             compiler_params=limit(4),
             name="pack",
-        )(queries[0], new_keys[0], new_values[0])
+        )(*(in_hbm(x[0]) for x in (queries, new_keys, new_values)))
         own = exchange(sent, same_core)
         other = lax.ppermute(own, "tp", across)
 
         block_rows = half_rs * local_heads + 2 * half_rs
         state = jax.ShapeDtypeStruct((2, chips, block_rows, HD), jnp.bfloat16)
-        keep, send = pl.pallas_call(
+        ints = (target_slot, page_owner, page_fill)
+        pages_shape = (tokens, key_pages.shape[3])
+        keys, values, bias_own, bias_moved = pl.pallas_call(
+            lambda *refs: prepare_kernel(steps, *refs),
+            out_shape=(
+                jax.ShapeDtypeStruct(pages_shape, key_pages.dtype),
+                jax.ShapeDtypeStruct(pages_shape, value_pages.dtype),
+                jax.ShapeDtypeStruct((row_steps, tokens), jnp.float32),
+                jax.ShapeDtypeStruct((GS * steps, tokens), jnp.float32),
+            ),
+            in_specs=[HBM] * 5 + [ANY],
+            out_specs=(VMEM,) * 4,
+            scratch_shapes=[
+                pltpu.SMEM(target_slot.shape, jnp.int32),
+                pltpu.VMEM(page_owner.shape, jnp.int32),
+                pltpu.VMEM(page_fill.shape, jnp.int32),
+                pltpu.SemaphoreType.DMA((5,)),
+            ],
+            compiler_params=limit(8),
+            name="prepare",
+        )(
+            *(in_hbm(x) for x in ints),
+            in_hbm(key_pages.reshape(pages_shape)),
+            in_hbm(value_pages.reshape(pages_shape)),
+            own,
+        )
+        weight_by_device = out_weight.reshape(width, features, out_weight.shape[1])
+        keep, send, weight = pl.pallas_call(
             lambda *refs: attend_kernel(chips, *refs),
-            out_shape=(state, state),
-            in_specs=[SMEM, SMEM] + [VMEM] * 6,
-            out_specs=(VMEM, VMEM),
-            scratch_shapes=[
-                pltpu.VMEM((row_steps, tokens), jnp.float32),
-                pltpu.VMEM((GS * steps, tokens), jnp.float32),
-            ],
-            compiler_params=limit(16),
+            out_shape=(
+                state,
+                state,
+                jax.ShapeDtypeStruct(weight_by_device.shape, weight_by_device.dtype),
+            ),
+            in_specs=[SMEM, SMEM] + [VMEM] * 6 + [HBM],
+            out_specs=(VMEM, VMEM, VMEM),
+            scratch_shapes=[pltpu.SemaphoreType.DMA((width,))],
+            compiler_params=limit(24),
             name="attend",
         )(
             info,
-            target_slot[0],
-            page_owner,
-            page_fill,
+            target_slot,
             own,
             other,
-            key_pages.reshape(tokens, key_pages.shape[3]),
-            value_pages.reshape(tokens, value_pages.shape[3]),
+            keys,
+            values,
+            bias_own,
+            bias_moved,
+            in_hbm(weight_by_device),
         )
         merged = pl.pallas_call(
             lambda *refs: merge_kernel(local_heads, *refs),
@@ -373,14 +485,22 @@
         )(info, arrived)
         own = exchange(finished.reshape(2 * chips, half_rs, features), same_core)
         other = lax.ppermute(own, "tp", across)
+        partial = pl.pallas_call(
+            lambda *refs: project_own_kernel(chips, *refs),
+            out_shape=jax.ShapeDtypeStruct((row_steps, out_weight.shape[1]), jnp.float32),
+            in_specs=[SMEM, VMEM, VMEM],
+            out_specs=VMEM,
+            compiler_params=limit(16),
+            name="project_own",
+        )(info, own, weight)
         projected = pl.pallas_call(
-            lambda *refs: project_kernel(chips, *refs),
+            lambda *refs: project_other_kernel(chips, *refs),
             out_shape=jax.ShapeDtypeStruct((rows, steps, out_weight.shape[1]), jnp.bfloat16),
             in_specs=[SMEM, VMEM, VMEM, VMEM],
             out_specs=VMEM,
             compiler_params=limit(16),
-            name="project",
-        )(info, own, other, out_weight.reshape(width, features, out_weight.shape[1]))
+            name="project_other",
+        )(info, partial, other, weight)
         return projected[None]
 
     return per_device

time: 68.8 us -> 58.9 us (0.86)
  local copies, waits for them, and re-layouts: 10.6 us -> 0.01 us
  Pallas kernels: 10.9 us -> 14.1 us
  waiting for transfers between devices: 4.2 us -> 1.23 us
    unnamed x18 -> x2, local copies, waits for them, and re-layouts: 10.6 us -> 0.01 us
    pallas_call x1 -> x3, Pallas kernels: 2.35 us -> 5.31 us  [the longest x1 2.31 us: per_device(): pl.pallas_call(lambda *refs: prepare_kernel(steps, *refs), out_shape=(jax...]
    ppermute x2, waiting for transfers between devices: 2.9 us -> 0.16 us  [per_device(): other = lax.ppermute(own, 'tp', across)]
    pallas_call x1, Pallas kernels: 0.09 us -> 0.83 us  [per_device(): pl.pallas_call(pack_kernel, out_shape=jax.ShapeDtypeStruct((2 * chips, ro...]
  transfers between devices with their start and end apart: 3 -> 3, of which waited for: 3 -> 2; matrix products, arithmetic and copies ran while one was open for 0% -> 0% of each run, Pallas kernels for 0% -> 6%
where the time goes in v4:
time: 58.9 us; the launch traced here: 58.6 us
  blocking collectives  42.6 us (72%)
  Pallas kernels  14.1 us (24%)
  waiting for transfers between devices  1.23 us (2%)
    all_to_all x3, blocking collectives, exchange(): return lax.all_to_all(x, both, 0, 0, axis_index_groups=members)  42.6 us
    pallas_call x1, Pallas kernels, per_device(): pl.pallas_call(lambda *refs: attend_kernel(chips, *refs), out_shape=(stat...  5.67 us
    pallas_call x1, Pallas kernels, per_device(): pl.pallas_call(lambda *refs: prepare_kernel(steps, *refs), out_shape=(jax...  2.31 us
    pallas_call x1, Pallas kernels, per_device(): pl.pallas_call(lambda *refs: project_other_kernel(chips, *refs), out_shap...  1.81 us
    pallas_call x1, Pallas kernels, per_device(): pl.pallas_call(lambda *refs: merge_kernel(local_heads, *refs), out_shape=...  1.22 us
    pallas_call x1, Pallas kernels, per_device(): pl.pallas_call(lambda *refs: project_own_kernel(chips, *refs), out_shape=...  1.19 us
  transfers between devices with their start and end apart: 3, of which 2 were waited for; matrix products, arithmetic and copies ran while one was open for 0% of the time, Pallas kernels for 6%

profile of v4, /device:TPU:0, one launch (start us, length us, event | category | flops | bytes accessed | tf_op | source)
XLA Modules:
  0.0 58.6 jit_solution(18234626046556303059)
XLA Ops:
  0.0 0.8 %pack.1 = bf16[16,16,640]{2,1,0:T(8,128)(2,1)S(1)} custom-call(bf16[8,2,512]{2,1,0:T(2,128)(2,1)} %bitcast.17, bf16[8,2,64]{2,1,0:T(2,128)(2,1)} %bitcast.18, bf16[8,2,64]{2,1,0:T(2,128)(2,1)} %bitcast.19), custom_call_target="tpu_custom_call" | custom-call | tf_op jit(solution)/shard_map/pack/pallas_call | solution.py:400
  0.8 19.5 %all_to_all.15.refs_5_.refs_2_ = bf16[16,16,640]{2,1,0:T(8,128)(2,1)S(1)} all-to-all(bf16[16,16,640]{2,1,0:T(8,128)(2,1)S(1)} %pack.1), channel_id=1, replica_groups={{0,2,4,6,8,10,12,14,16,18,20,22,24,26,28,30},{1,3,5,7,9,11,13,15,17,19,..., dimensions={0} | all-to-all | bytes 655360 | tf_op jit(solution)/shard_map/all_to_all | solution.py:377
  20.3 0.0 collective-permute-start
  20.3 0.1 pad_add_fusion.refs_0_
  20.4 0.0 copy-start
  20.4 2.3 %prepare.1 = (bf16[1024,1024]{1,0:T(8,128)(2,1)S(1)}, bf16[1024,1024]{1,0:T(8,128)(2,1)S(1)}, f32[16,1024]{1,0:T(8,128)S(1)}, f32[16,1024]{1,0:T(8,128)S(1)}) custom-call(s32[1,8]{1,0:T(1,128)} %refs_1_.3, s32[1,64]{1,0:T(1,128)} %refs_1_.2, s32[1,64]{1,0:T(1,128)} %refs_2_.1, bf16[1024,1024]{1,0:T(8,128)(2,1)} %bitcast.15, bf16[1024,1024]{1,0:T(8,128)(2,1)} %bitcast.16, ...), custom_call_target="tpu_custom_call" | custom-call | tf_op jit(solution)/shard_map/prepare/pallas_call | solution.py:421
  22.7 0.0 collective-permute-done.refs_3_
  22.7 0.0 copy-done
  22.7 5.7 %attend.1 = (bf16[2,8,48,128]{3,2,1,0:T(8,128)(2,1)S(1)}, bf16[2,8,48,128]{3,2,1,0:T(8,128)(2,1)S(1)}, bf16[16,512,512]{2,1,0:T(8,128)(2,1)S(1)}) custom-call(s32[3]{0:T(128)S(1)} %pad_add_fusion.refs_0_, s32[1,8]{1,0:T(1,128)S(1)} %copy-done, bf16[16,16,640]{2,1,0:T(8,128)(2,1)S(1)} %all_to_all.15.refs_5_.refs_2_, ...), custom_call_target="tpu_custom_call" | custom-call | tf_op jit(solution)/shard_map/attend/pallas_call | solution.py:446
  28.4 0.6 collective-permute-start.1
  29.0 1.1 %collective-permute-done.1.refs_1_ = bf16[2,8,48,128]{3,2,1,0:T(8,128)(2,1)S(1)} collective-permute-done((bf16[2,8,48,128]{3,2,1,0:T(8,128)(2,1)S(1)}, bf16[2,8,48,128]{3,2,1,0:T(8,128)(2,1)S(1)}, u32[]{:S(2)}, u32[]{:S(2)}) %collective-permute-start.1) | collective-permute-done | bytes 196640 | tf_op jit(solution)/shard_map/ppermute | solution.py:476
  30.0 1.2 %merge.1 = bf16[2,8,48,128]{3,2,1,0:T(8,128)(2,1)S(1)} custom-call(bf16[2,8,48,128]{3,2,1,0:T(8,128)(2,1)S(1)} %get-tuple-element.16.refs_0_, bf16[2,8,48,128]{3,2,1,0:T(8,128)(2,1)S(1)} %collective-permute-done.1.refs_1_), custom_call_target="tpu_custom_call" | custom-call | tf_op jit(solution)/shard_map/merge/pallas_call | solution.py:469
  31.3 12.0 %all_to_all.16.refs_1_ = bf16[16,48,128]{2,1,0:T(8,128)(2,1)S(1)} all-to-all(bf16[16,48,128]{2,1,0:T(8,128)(2,1)S(1)} %bitcast.12), channel_id=1, replica_groups={{0,2,4,6,8,10,12,14,16,18,20,22,24,26,28,30},{1,3,5,7,9,11,13,15,17,19,..., dimensions={0} | all-to-all | bytes 393216 | tf_op jit(solution)/shard_map/all_to_all | solution.py:377
  43.3 1.0 %reduce.1 = bf16[2,8,8,512]{3,2,1,0:T(8,128)(2,1)S(1)} custom-call(s32[3]{0:T(128)S(1)} %pad_add_fusion.refs_0_, bf16[16,48,128]{2,1,0:T(8,128)(2,1)S(1)} %all_to_all.16.refs_1_), custom_call_target="tpu_custom_call" | custom-call | tf_op jit(solution)/shard_map/reduce/pallas_call | solution.py:478
  44.3 11.1 %all_to_all.17.refs_1_ = bf16[16,8,512]{2,1,0:T(8,128)(2,1)S(1)} all-to-all(bf16[16,8,512]{2,1,0:T(8,128)(2,1)S(1)} %bitcast.13), channel_id=1, replica_groups={{0,2,4,6,8,10,12,14,16,18,20,22,24,26,28,30},{1,3,5,7,9,11,13,15,17,19,..., dimensions={0} | all-to-all | bytes 262144 | tf_op jit(solution)/shard_map/all_to_all | solution.py:377
  55.4 0.0 collective-permute-start.2
  55.4 1.2 %project_own.1.refs_1_ = f32[16,512]{1,0:T(8,128)S(1)} custom-call(s32[3]{0:T(128)S(1)} %pad_add_fusion.refs_0_, bf16[16,8,512]{2,1,0:T(8,128)(2,1)S(1)} %all_to_all.17.refs_1_, bf16[16,512,512]{2,1,0:T(8,128)(2,1)S(1)} %get-tuple-element.18.refs_2_.refs_3_), custom_call_target="tpu_custom_call" | custom-call | tf_op jit(solution)/shard_map/project_own/pallas_call | solution.py:488
  56.6 0.2 collective-permute-done.2.refs_2_
  56.7 1.8 %project_other.1 = bf16[8,2,512]{2,1,0:T(2,128)(2,1)} custom-call(s32[3]{0:T(128)S(1)} %pad_add_fusion.refs_0_, f32[16,512]{1,0:T(8,128)S(1)} %project_own.1.refs_1_, bf16[16,8,512]{2,1,0:T(8,128)(2,1)S(1)} %collective-permute-done.2.refs_2_, bf16[16,512,512]{2,1,0:T(8,128)(2,1)S(1)} %get-tuple-element.18.refs_2_.refs_3_), custom_call_target="tpu_custom_call" | custom-call | tf_op jit(solution)/shard_map/project_other/pallas_call | solution.py:496
Async XLA Ops:
  20.3 2.4 %collective-permute-start = (bf16[16,16,640]{2,1,0:T(8,128)(2,1)S(1)}, bf16[16,16,640]{2,1,0:T(8,128)(2,1)S(1)}, u32[]{:S(2)}, u32[]{:S(2)}) collective-permute-start(bf16[16,16,640]{2,1,0:T(8,128)(2,1)S(1)} %all_to_all.15.refs_5_.refs_2_), channel_id=1, source_target_pairs={{0,1},{1,0},{2,3},{3,2},{4,5},{5,4},{6,7},{7,6},{8,9},{9,8},{10,11... | collective-permute-start | bytes 983048 | tf_op jit(solution)/shard_map/ppermute | solution.py:415
  20.4 2.3 %copy-start = (s32[1,8]{1,0:T(1,128)S(1)}, s32[1,8]{1,0:T(1,128)}, u32[]{:S(2)}) copy-start(s32[1,8]{1,0:T(1,128)} %refs_1_.3) | copy-start | bytes 100
  28.4 1.6 %collective-permute-start.1 = (bf16[2,8,48,128]{3,2,1,0:T(8,128)(2,1)S(1)}, bf16[2,8,48,128]{3,2,1,0:T(8,128)(2,1)S(1)}, u32[]{:S(2)}, u32[]{:S(2)}) collective-permute-start(bf16[2,8,48,128]{3,2,1,0:T(8,128)(2,1)S(1)} %get-tuple-element.17), channel_id=1, source_target_pairs={{0,1},{1,0},{2,3},{3,2},{4,5},{5,4},{6,7},{7,6},{8,9},{9,8},{10,11... | collective-permute-start | bytes 589832 | tf_op jit(solution)/shard_map/ppermute | solution.py:476
  55.4 1.3 %collective-permute-start.2 = (bf16[16,8,512]{2,1,0:T(8,128)(2,1)S(1)}, bf16[16,8,512]{2,1,0:T(8,128)(2,1)S(1)}, u32[]{:S(2)}, u32[]{:S(2)}) collective-permute-start(bf16[16,8,512]{2,1,0:T(8,128)(2,1)S(1)} %all_to_all.17.refs_1_), channel_id=1, source_target_pairs={{0,1},{1,0},{2,3},{3,2},{4,5},{5,4},{6,7},{7,6},{8,9},{9,8},{10,11... | collective-permute-start | bytes 393224 | tf_op jit(solution)/shard_map/ppermute | solution.py:487

commit v5 on v4

--- a/solution.py
+++ b/solution.py
@@ -17,7 +17,7 @@
 MOVED_LANE = 64
 TARGET_LANE = 127
 GS = HEADS // KVH
-UNROLL = 2
+UNROLL = 4
 
 
 def dot(a, b, contract):
@@ -28,7 +28,7 @@
     return lax.broadcasted_iota(jnp.int32, shape, axis)
 
 
-def pack_kernel(queries, new_keys, new_values, out, q_buf, k_buf, v_buf, sems):
+def pack_kernel(queries, new_keys, new_values, out, new_out, q_buf, k_buf, v_buf, sems):
     row_steps = out.shape[1]
     buffers = (q_buf, k_buf, v_buf)
     copies = [
@@ -39,9 +39,10 @@
         c.start()
     for c in copies:
         c.wait()
-    row = jnp.concatenate([b[...].reshape(row_steps, b.shape[2]) for b in buffers], axis=1)
+    rows = [b[...].reshape(row_steps, b.shape[2]) for b in buffers]
     for i in range(out.shape[0]):
-        out[i] = row
+        out[i] = rows[0]
+    new_out[...] = jnp.concatenate(rows[1:], axis=1)
 
 
 def sums_of(aux, local_heads):
@@ -123,21 +124,19 @@
     bias_own,
     bias_moved,
     weight_hbm,
-    keep,
-    send,
-    weight,
-    weight_sems,
+    *rest,
 ):
+    *new_tokens, keep, send, weight, weight_sems = rest
     row_steps = own.shape[1]
     steps = row_steps // slots.shape[1]
     features = HEADS // (2 * chips) * HD
     local_heads = features // HD
-    kv_part = (own.shape[2] - features) // 2
+    kv_part = new_tokens[0].shape[1] // 2
     per_kv = chips // KVH
     half_rs = row_steps // 2
     half = info[0]
-    core = info[1]
-    first = info[2]
+    spot = info[2]
+    own_kv = info[3]
     _, target = mover_of(slots)
     copies = [
         pltpu.make_async_copy(weight_hbm.at[i], weight.at[i], weight_sems.at[i])
@@ -149,7 +148,15 @@
     rs_ids = iota((row_steps, row_steps), 0)
     new_ids = iota((row_steps, row_steps), 1)
     new_live = (rs_ids // steps == new_ids // steps) & (new_ids % steps <= rs_ids % steps)
-    bias_new = jnp.where(new_live & (first == 1), 0.0, NEG)
+    bias_new = jnp.where(new_live & (spot == 0), 0.0, NEG)
+    pieces = []
+    for p in range(len(new_tokens)):
+        piece = new_tokens[0][...].astype(jnp.float32)
+        for i in range(1, len(new_tokens)):
+            piece = jnp.where(spot == p ^ i, new_tokens[i][...].astype(jnp.float32), piece)
+        pieces.append(piece)
+    new_k = jnp.concatenate([x[:, :kv_part] for x in pieces], axis=1).astype(jnp.bfloat16)
+    new_v = jnp.concatenate([x[:, kv_part:] for x in pieces], axis=1).astype(jnp.bfloat16)
     moved_rows = GS * steps
     wide = GS * row_steps
     pick_ids = iota((moved_rows, wide), 0)
@@ -161,7 +168,7 @@
     target_f = target.astype(jnp.float32)
 
     def per_head(g, carry):
-        tiles, partner_tiles, new_k, new_v = [], [], [], []
+        tiles, partner_tiles = [], []
         for source in (own, other):
             for kl in range(per_kv):
                 mine = source[half * chips + g * per_kv + kl]
@@ -169,19 +176,6 @@
                 for j in range(local_heads):
                     tiles.append(mine[:, j * HD : (j + 1) * HD])
                     partner_tiles.append(theirs[:, j * HD : (j + 1) * HD])
-                new_k.append(mine[:, features : features + kv_part])
-                new_v.append(mine[:, features + kv_part :])
-
-        def in_order(parts):
-            mine, theirs = parts[:per_kv], parts[per_kv:]
-            a = [x for pair in zip(mine, theirs) for x in pair]
-            b = [x for pair in zip(theirs, mine) for x in pair]
-            return jnp.where(
-                core == 0,
-                jnp.concatenate(a, axis=1).astype(jnp.float32),
-                jnp.concatenate(b, axis=1).astype(jnp.float32),
-            ).astype(jnp.bfloat16)
-
         moved_q = dot(pick, jnp.concatenate(partner_tiles, axis=0), ((1,), (0,)))
         q = jnp.concatenate(tiles + [moved_q.astype(jnp.bfloat16)], axis=0)
         at = pl.ds(pl.multiple_of(g * HD, HD), HD)
@@ -190,8 +184,9 @@
         scores = dot(q, k, ((1,), (1,))) * SCALE
         bias = jnp.concatenate([bias_own[...]] * GS + [bias_moved[...]], axis=0)
         scores = scores + bias
-        new_scores = dot(q[:wide], in_order(new_k), ((1,), (1,))) * SCALE
-        new_scores = new_scores + jnp.concatenate([bias_new] * GS, axis=0)
+        new_scores = dot(q[:wide], new_k, ((1,), (1,))) * SCALE
+        bias = jnp.where(g == own_kv, bias_new, NEG)
+        new_scores = new_scores + jnp.concatenate([bias] * GS, axis=0)
         new_scores = jnp.concatenate(
             [new_scores, jnp.full((moved_rows, row_steps), NEG, jnp.float32)], axis=0
         )
@@ -204,8 +199,8 @@
         total = jnp.sum(p.astype(jnp.float32), axis=1, keepdims=True) + jnp.sum(
             pn.astype(jnp.float32), axis=1, keepdims=True
         )
-        acc = dot(p, v, ((1,), (0,))) + dot(pn, in_order(new_v), ((1,), (0,)))
-        high, low = split(total)
+        acc = dot(p, v, ((1,), (0,))) + dot(pn, new_v, ((1,), (0,)))
+        top_part, low_part = split(total)
 
         for side in range(2):
             for kl in range(per_kv):
@@ -225,8 +220,8 @@
                         for j in range(local_heads)
                     ]
                     aux = jnp.where(lane == MOVED_LANE, filled(top[at_moved]), 0.0)
-                    aux = jnp.where(lane == MOVED_LANE + local_heads, filled(high[at_moved]), aux)
-                    aux = jnp.where(lane == MOVED_LANE + 2 * local_heads, filled(low[at_moved]), aux)
+                    aux = jnp.where(lane == MOVED_LANE + local_heads, filled(top_part[at_moved]), aux)
+                    aux = jnp.where(lane == MOVED_LANE + 2 * local_heads, filled(low_part[at_moved]), aux)
                     aux = jnp.where(lane == TARGET_LANE, target_f, aux)
                     for j in range(local_heads):
                         rows_at = slice(
@@ -234,8 +229,8 @@
                             (t0 + j) * row_steps + (h + 1) * half_rs,
                         )
                         aux = jnp.where(lane == j, top[rows_at], aux)
-                        aux = jnp.where(lane == local_heads + j, high[rows_at], aux)
-                        aux = jnp.where(lane == 2 * local_heads + j, low[rows_at], aux)
+                        aux = jnp.where(lane == local_heads + j, top_part[rows_at], aux)
+                        aux = jnp.where(lane == 2 * local_heads + j, low_part[rows_at], aux)
                     block = jnp.concatenate(parts + [filled(moved_acc), aux], axis=0)
                     dest = keep if side == 0 else send
                     dest[h, g * per_kv + kl] = block.astype(jnp.bfloat16)
@@ -395,15 +390,18 @@
         tokens = pages * PAGE
         place = lax.axis_index("tp")
         half = lax.axis_index("group") // apart
-        info = jnp.stack([half, place & 1, (place == 0).astype(jnp.int32)]).astype(jnp.int32)
-
-        sent = pl.pallas_call(
+        spread = width // KVH
+        info = jnp.stack([half, place & 1, place & (spread - 1), place // spread])
+        info = info.astype(jnp.int32)
+
+        sent, new_own = pl.pallas_call(
             pack_kernel,
-            out_shape=jax.ShapeDtypeStruct(
-                (2 * chips, row_steps, features + 2 * new_keys.shape[3]), jnp.bfloat16
+            out_shape=(
+                jax.ShapeDtypeStruct((2 * chips, row_steps, features), jnp.bfloat16),
+                jax.ShapeDtypeStruct((row_steps, 2 * new_keys.shape[3]), jnp.bfloat16),
             ),
             in_specs=[HBM] * 3,
-            out_specs=VMEM,
+            out_specs=(VMEM, VMEM),
             scratch_shapes=[
                 pltpu.VMEM(x.shape[1:], x.dtype) for x in (queries, new_keys, new_values)
             ]
@@ -411,6 +409,10 @@
             compiler_params=limit(4),
             name="pack",
         )(*(in_hbm(x[0]) for x in (queries, new_keys, new_values)))
+        new_tokens = [new_own] + [
+            lax.ppermute(new_own, "tp", [(t, t ^ i) for t in range(width)])
+            for i in range(1, spread)
+        ]
         own = exchange(sent, same_core)
         other = lax.ppermute(own, "tp", across)
 
@@ -450,7 +452,7 @@
                 state,
                 jax.ShapeDtypeStruct(weight_by_device.shape, weight_by_device.dtype),
             ),
-            in_specs=[SMEM, SMEM] + [VMEM] * 6 + [HBM],
+            in_specs=[SMEM, SMEM] + [VMEM] * 6 + [HBM] + [VMEM] * spread,
             out_specs=(VMEM, VMEM, VMEM),
             scratch_shapes=[pltpu.SemaphoreType.DMA((width,))],
             compiler_params=limit(24),
@@ -465,6 +467,7 @@
             bias_own,
             bias_moved,
             in_hbm(weight_by_device),
+            *new_tokens,
         )
         merged = pl.pallas_call(
             lambda *refs: merge_kernel(local_heads, *refs),

time: 58.9 us -> 57.3 us (0.973)
  blocking collectives: 42.6 us -> 41 us
    all_to_all x3, blocking collectives: 42.6 us -> 41 us  [exchange(): return lax.all_to_all(x, both, 0, 0, axis_index_groups=members)]
  transfers between devices with their start and end apart: 3 -> 4, of which waited for: 2 -> 2; matrix products, arithmetic and copies ran while one was open for 0% -> 0% of each run, Pallas kernels for 6% -> 6%
where the time goes in v5:
time: 57.3 us; the launch traced here: 56.9 us
  blocking collectives  41 us (72%)
  Pallas kernels  13.7 us (24%)
  waiting for transfers between devices  1.59 us (3%)
  starting transfers between devices  0.58 us (1%)
    all_to_all x3, blocking collectives, exchange(): return lax.all_to_all(x, both, 0, 0, axis_index_groups=members)  41 us
    pallas_call x1, Pallas kernels, per_device(): pl.pallas_call(lambda *refs: attend_kernel(chips, *refs), out_shape=(stat...  5.29 us
    pallas_call x1, Pallas kernels, per_device(): pl.pallas_call(lambda *refs: prepare_kernel(steps, *refs), out_shape=(jax...  2.31 us
    pallas_call x1, Pallas kernels, per_device(): pl.pallas_call(lambda *refs: project_other_kernel(chips, *refs), out_shap...  1.81 us
    ppermute x1, waiting for transfers between devices, per_device(): lax.ppermute(send, 'tp', across)  1.43 us
    pallas_call x1, Pallas kernels, per_device(): pl.pallas_call(lambda *refs: merge_kernel(local_heads, *refs), out_shape=...  1.22 us
    pallas_call x1, Pallas kernels, per_device(): pl.pallas_call(lambda *refs: project_own_kernel(chips, *refs), out_shape=...  1.19 us
  transfers between devices with their start and end apart: 4, of which 2 were waited for; matrix products, arithmetic and copies ran while one was open for 0% of the time, Pallas kernels for 6%

profile of v5, /device:TPU:0, one launch (start us, length us, event | category | flops | bytes accessed | tf_op | source)
XLA Modules:
  0.0 56.9 jit_solution(10708229732906762511)
XLA Ops:
  0.0 0.8 %pack.1 = (bf16[16,16,512]{2,1,0:T(8,128)(2,1)S(1)}, bf16[16,128]{1,0:T(8,128)(2,1)S(1)}) custom-call(bf16[8,2,512]{2,1,0:T(2,128)(2,1)} %bitcast.17, bf16[8,2,64]{2,1,0:T(2,128)(2,1)} %bitcast.18, bf16[8,2,64]{2,1,0:T(2,128)(2,1)} %bitcast.19), custom_call_target="tpu_custom_call" | custom-call | tf_op jit(solution)/shard_map/pack/pallas_call | solution.py:397
  0.8 18.0 %all_to_all.15.refs_5_.refs_2_ = bf16[16,16,512]{2,1,0:T(8,128)(2,1)S(1)} all-to-all(bf16[16,16,512]{2,1,0:T(8,128)(2,1)S(1)} %get-tuple-element.14), channel_id=1, replica_groups={{0,2,4,6,8,10,12,14,16,18,20,22,24,26,28,30},{1,3,5,7,9,11,13,15,17,19,..., dimensions={0} | all-to-all | bytes 524288 | tf_op jit(solution)/shard_map/all_to_all | solution.py:372
  18.8 0.0 collective-permute-start
  18.8 0.5 collective-permute-start.1
  19.4 0.1 pad_add_fusion.refs_0_
  19.4 0.0 copy-start
  19.4 2.3 %prepare.1 = (bf16[1024,1024]{1,0:T(8,128)(2,1)S(1)}, bf16[1024,1024]{1,0:T(8,128)(2,1)S(1)}, f32[16,1024]{1,0:T(8,128)S(1)}, f32[16,1024]{1,0:T(8,128)S(1)}) custom-call(s32[1,8]{1,0:T(1,128)} %refs_1_.3, s32[1,64]{1,0:T(1,128)} %refs_1_.2, s32[1,64]{1,0:T(1,128)} %refs_2_.1, bf16[1024,1024]{1,0:T(8,128)(2,1)} %bitcast.15, bf16[1024,1024]{1,0:T(8,128)(2,1)} %bitcast.16, ...), custom_call_target="tpu_custom_call" | custom-call | tf_op jit(solution)/shard_map/prepare/pallas_call | solution.py:423
  21.8 0.0 collective-permute-done.1.refs_10_
  21.8 0.0 collective-permute-done.refs_3_
  21.8 0.0 copy-done
  21.8 5.3 %attend.1 = (bf16[2,8,48,128]{3,2,1,0:T(8,128)(2,1)S(1)}, bf16[2,8,48,128]{3,2,1,0:T(8,128)(2,1)S(1)}, bf16[16,512,512]{2,1,0:T(8,128)(2,1)S(1)}) custom-call(s32[4]{0:T(128)S(1)} %pad_add_fusion.refs_0_, s32[1,8]{1,0:T(1,128)S(1)} %copy-done, bf16[16,16,512]{2,1,0:T(8,128)(2,1)S(1)} %all_to_all.15.refs_5_.refs_2_, ...), custom_call_target="tpu_custom_call" | custom-call | tf_op jit(solution)/shard_map/attend/pallas_call | solution.py:448
  27.1 0.1 collective-permute-start.2
  27.2 1.4 %collective-permute-done.2.refs_1_ = bf16[2,8,48,128]{3,2,1,0:T(8,128)(2,1)S(1)} collective-permute-done((bf16[2,8,48,128]{3,2,1,0:T(8,128)(2,1)S(1)}, bf16[2,8,48,128]{3,2,1,0:T(8,128)(2,1)S(1)}, u32[]{:S(2)}, u32[]{:S(2)}) %collective-permute-start.2) | collective-permute-done | bytes 196640 | tf_op jit(solution)/shard_map/ppermute | solution.py:479
  28.6 1.2 %merge.1 = bf16[2,8,48,128]{3,2,1,0:T(8,128)(2,1)S(1)} custom-call(bf16[2,8,48,128]{3,2,1,0:T(8,128)(2,1)S(1)} %get-tuple-element.20.refs_0_, bf16[2,8,48,128]{3,2,1,0:T(8,128)(2,1)S(1)} %collective-permute-done.2.refs_1_), custom_call_target="tpu_custom_call" | custom-call | tf_op jit(solution)/shard_map/merge/pallas_call | solution.py:472
  29.8 11.9 %all_to_all.16.refs_1_ = bf16[16,48,128]{2,1,0:T(8,128)(2,1)S(1)} all-to-all(bf16[16,48,128]{2,1,0:T(8,128)(2,1)S(1)} %bitcast.12), channel_id=1, replica_groups={{0,2,4,6,8,10,12,14,16,18,20,22,24,26,28,30},{1,3,5,7,9,11,13,15,17,19,..., dimensions={0} | all-to-all | bytes 393216 | tf_op jit(solution)/shard_map/all_to_all | solution.py:372
  41.7 1.0 %reduce.1 = bf16[2,8,8,512]{3,2,1,0:T(8,128)(2,1)S(1)} custom-call(s32[4]{0:T(128)S(1)} %pad_add_fusion.refs_0_, bf16[16,48,128]{2,1,0:T(8,128)(2,1)S(1)} %all_to_all.16.refs_1_), custom_call_target="tpu_custom_call" | custom-call | tf_op jit(solution)/shard_map/reduce/pallas_call | solution.py:481
  42.7 11.1 %all_to_all.17.refs_1_ = bf16[16,8,512]{2,1,0:T(8,128)(2,1)S(1)} all-to-all(bf16[16,8,512]{2,1,0:T(8,128)(2,1)S(1)} %bitcast.13), channel_id=1, replica_groups={{0,2,4,6,8,10,12,14,16,18,20,22,24,26,28,30},{1,3,5,7,9,11,13,15,17,19,..., dimensions={0} | all-to-all | bytes 262144 | tf_op jit(solution)/shard_map/all_to_all | solution.py:372
  53.8 0.0 collective-permute-start.3
  53.8 1.2 %project_own.1.refs_1_ = f32[16,512]{1,0:T(8,128)S(1)} custom-call(s32[4]{0:T(128)S(1)} %pad_add_fusion.refs_0_, bf16[16,8,512]{2,1,0:T(8,128)(2,1)S(1)} %all_to_all.17.refs_1_, bf16[16,512,512]{2,1,0:T(8,128)(2,1)S(1)} %get-tuple-element.22.refs_2_.refs_3_), custom_call_target="tpu_custom_call" | custom-call | tf_op jit(solution)/shard_map/project_own/pallas_call | solution.py:491
  55.0 0.2 collective-permute-done.3.refs_2_
  55.1 1.8 %project_other.1 = bf16[8,2,512]{2,1,0:T(2,128)(2,1)} custom-call(s32[4]{0:T(128)S(1)} %pad_add_fusion.refs_0_, f32[16,512]{1,0:T(8,128)S(1)} %project_own.1.refs_1_, bf16[16,8,512]{2,1,0:T(8,128)(2,1)S(1)} %collective-permute-done.3.refs_2_, bf16[16,512,512]{2,1,0:T(8,128)(2,1)S(1)} %get-tuple-element.22.refs_2_.refs_3_), custom_call_target="tpu_custom_call" | custom-call | tf_op jit(solution)/shard_map/project_other/pallas_call | solution.py:499
Async XLA Ops:
  18.8 2.9 %collective-permute-start = (bf16[16,16,512]{2,1,0:T(8,128)(2,1)S(1)}, bf16[16,16,512]{2,1,0:T(8,128)(2,1)S(1)}, u32[]{:S(2)}, u32[]{:S(2)}) collective-permute-start(bf16[16,16,512]{2,1,0:T(8,128)(2,1)S(1)} %all_to_all.15.refs_5_.refs_2_), channel_id=1, source_target_pairs={{0,1},{1,0},{2,3},{3,2},{4,5},{5,4},{6,7},{7,6},{8,9},{9,8},{10,11... | collective-permute-start | bytes 786440 | tf_op jit(solution)/shard_map/ppermute | solution.py:417
  18.8 2.9 %collective-permute-start.1 = (bf16[16,128]{1,0:T(8,128)(2,1)S(1)}, bf16[16,128]{1,0:T(8,128)(2,1)S(1)}, u32[]{:S(2)}, u32[]{:S(2)}) collective-permute-start(bf16[16,128]{1,0:T(8,128)(2,1)S(1)} %get-tuple-element.19.refs_9_), channel_id=1, source_target_pairs={{0,1},{1,0},{2,3},{3,2},{4,5},{5,4},{6,7},{7,6},{8,9},{9,8},{10,11... | collective-permute-start | bytes 12296 | tf_op jit(solution)/shard_map/ppermute | solution.py:413
  19.4 2.3 %copy-start = (s32[1,8]{1,0:T(1,128)S(1)}, s32[1,8]{1,0:T(1,128)}, u32[]{:S(2)}) copy-start(s32[1,8]{1,0:T(1,128)} %refs_1_.3) | copy-start | bytes 100
  27.1 1.5 %collective-permute-start.2 = (bf16[2,8,48,128]{3,2,1,0:T(8,128)(2,1)S(1)}, bf16[2,8,48,128]{3,2,1,0:T(8,128)(2,1)S(1)}, u32[]{:S(2)}, u32[]{:S(2)}) collective-permute-start(bf16[2,8,48,128]{3,2,1,0:T(8,128)(2,1)S(1)} %get-tuple-element.21), channel_id=1, source_target_pairs={{0,1},{1,0},{2,3},{3,2},{4,5},{5,4},{6,7},{7,6},{8,9},{9,8},{10,11... | collective-permute-start | bytes 589832 | tf_op jit(solution)/shard_map/ppermute | solution.py:479
  53.8 1.3 %collective-permute-start.3 = (bf16[16,8,512]{2,1,0:T(8,128)(2,1)S(1)}, bf16[16,8,512]{2,1,0:T(8,128)(2,1)S(1)}, u32[]{:S(2)}, u32[]{:S(2)}) collective-permute-start(bf16[16,8,512]{2,1,0:T(8,128)(2,1)S(1)} %all_to_all.17.refs_1_), channel_id=1, source_target_pairs={{0,1},{1,0},{2,3},{3,2},{4,5},{5,4},{6,7},{7,6},{8,9},{9,8},{10,11... | collective-permute-start | bytes 393224 | tf_op jit(solution)/shard_map/ppermute | solution.py:490

commit v6 on v5

--- a/solution.py
+++ b/solution.py
@@ -17,7 +17,10 @@
 MOVED_LANE = 64
 TARGET_LANE = 127
 GS = HEADS // KVH
-UNROLL = 4
+UNROLL = 2
+TOGETHER = 2
+MERGE_UNROLL = 4
+REDUCE_UNROLL = 2
 
 
 def dot(a, b, contract):
@@ -167,7 +170,12 @@
     lane = iota((half_rs, HD), 1)
     target_f = target.astype(jnp.float32)
 
-    def per_head(g, carry):
+    pad = HD - row_steps
+    new_k = jnp.concatenate([new_k, jnp.zeros((pad, HD), new_k.dtype)], axis=0)
+    new_v = jnp.concatenate([new_v, jnp.zeros((pad, HD), new_v.dtype)], axis=0)
+    bias_new = jnp.concatenate([bias_new, jnp.full((row_steps, pad), NEG, jnp.float32)], axis=1)
+
+    def gather(g):
         tiles, partner_tiles = [], []
         for source in (own, other):
             for kl in range(per_kv):
@@ -177,31 +185,28 @@
                     tiles.append(mine[:, j * HD : (j + 1) * HD])
                     partner_tiles.append(theirs[:, j * HD : (j + 1) * HD])
         moved_q = dot(pick, jnp.concatenate(partner_tiles, axis=0), ((1,), (0,)))
-        q = jnp.concatenate(tiles + [moved_q.astype(jnp.bfloat16)], axis=0)
-        at = pl.ds(pl.multiple_of(g * HD, HD), HD)
-        k = keys[:, at]
-        v = values[:, at]
-        scores = dot(q, k, ((1,), (1,))) * SCALE
-        bias = jnp.concatenate([bias_own[...]] * GS + [bias_moved[...]], axis=0)
-        scores = scores + bias
-        new_scores = dot(q[:wide], new_k, ((1,), (1,))) * SCALE
-        bias = jnp.where(g == own_kv, bias_new, NEG)
-        new_scores = new_scores + jnp.concatenate([bias] * GS, axis=0)
-        new_scores = jnp.concatenate(
-            [new_scores, jnp.full((moved_rows, row_steps), NEG, jnp.float32)], axis=0
-        )
-        top = jnp.maximum(
-            jnp.max(scores, axis=1, keepdims=True), jnp.max(new_scores, axis=1, keepdims=True)
-        )
+        return jnp.concatenate(tiles + [moved_q.astype(jnp.bfloat16)], axis=0)
+
+    def score(g, q):
+        k = keys[:, pl.ds(pl.multiple_of(g * HD, HD), HD)]
+        scores = dot(q, jnp.concatenate([k, new_k], axis=0), ((1,), (1,))) * SCALE
+        extra = jnp.where(g == own_kv, bias_new, NEG)
+        bias_rows = jnp.concatenate([bias_own[...], extra], axis=1)
+        moved = jnp.concatenate([bias_moved[...], jnp.full((moved_rows, HD), NEG)], axis=1)
+        return scores + jnp.concatenate([bias_rows] * GS + [moved], axis=0)
+
+    def weigh(scores):
+        top = jnp.max(scores, axis=1, keepdims=True)
         top = jnp.maximum(top, FLOOR).astype(jnp.bfloat16).astype(jnp.float32)
         p = jnp.exp2(scores - top).astype(jnp.bfloat16)
-        pn = jnp.exp2(new_scores - top).astype(jnp.bfloat16)
-        total = jnp.sum(p.astype(jnp.float32), axis=1, keepdims=True) + jnp.sum(
-            pn.astype(jnp.float32), axis=1, keepdims=True
-        )
-        acc = dot(p, v, ((1,), (0,))) + dot(pn, new_v, ((1,), (0,)))
+        return top, p, jnp.sum(p.astype(jnp.float32), axis=1, keepdims=True)
+
+    def combine(g, p):
+        v = values[:, pl.ds(pl.multiple_of(g * HD, HD), HD)]
+        return dot(p, jnp.concatenate([v, new_v], axis=0), ((1,), (0,)))
+
+    def emit(g, top, total, acc):
         top_part, low_part = split(total)
-
         for side in range(2):
             for kl in range(per_kv):
                 t0 = (side * per_kv + kl) * local_heads
@@ -234,9 +239,17 @@
                     block = jnp.concatenate(parts + [filled(moved_acc), aux], axis=0)
                     dest = keep if side == 0 else send
                     dest[h, g * per_kv + kl] = block.astype(jnp.bfloat16)
+
+    def some_heads(i, carry):
+        heads = [i * TOGETHER + n for n in range(TOGETHER)]
+        scores = [score(g, q) for g, q in zip(heads, [gather(g) for g in heads])]
+        weighed = [weigh(x) for x in scores]
+        accs = [combine(g, w[1]) for g, w in zip(heads, weighed)]
+        for g, w, acc in zip(heads, weighed, accs):
+            emit(g, w[0], w[2], acc)
         return carry
 
-    lax.fori_loop(0, KVH, per_head, 0, unroll=UNROLL)
+    lax.fori_loop(0, KVH // TOGETHER, some_heads, 0, unroll=UNROLL)
     for c in copies:
         c.wait()
 
@@ -245,28 +258,33 @@
     half_rs = (first.shape[2]) // (local_heads + 2)
     span = half_rs * local_heads
     lane = iota((half_rs, HD), 1)
-    for h in range(first.shape[0]):
-        for k in range(first.shape[1]):
-            a = first[h, k].astype(jnp.float32)
-            b = second[h, k].astype(jnp.float32)
-            aux_a, aux_b = a[span + half_rs :], b[span + half_rs :]
-            top = jnp.maximum(aux_a, aux_b)
-            wa = jnp.exp2(aux_a - top)
-            wb = jnp.exp2(aux_b - top)
-            total = wa * sums_of(aux_a, local_heads) + wb * sums_of(aux_b, local_heads)
-            high, low = split(total)
-            is_top = (lane < local_heads) | (lane >= MOVED_LANE)
-            is_top = is_top & (lane < MOVED_LANE + local_heads) | (lane == TARGET_LANE)
-            high = pltpu.roll(high, local_heads, 1)
-            low = pltpu.roll(low, 2 * local_heads, 1)
-            part = lane % MOVED_LANE // local_heads
-            aux = jnp.where(is_top, top, jnp.where(part == 1, high, low))
-            parts = []
-            for j in range(local_heads + 1):
-                at = j if j < local_heads else MOVED_LANE
-                rows = slice(j * half_rs, (j + 1) * half_rs)
-                parts.append(wa[:, at : at + 1] * a[rows] + wb[:, at : at + 1] * b[rows])
-            out[h, k] = jnp.concatenate(parts + [aux], axis=0).astype(jnp.bfloat16)
+    chips = first.shape[1]
+
+    def one(i, carry):
+        h, k = i // chips, lax.rem(i, chips)
+        a = first[h, k].astype(jnp.float32)
+        b = second[h, k].astype(jnp.float32)
+        aux_a, aux_b = a[span + half_rs :], b[span + half_rs :]
+        top = jnp.maximum(aux_a, aux_b)
+        wa = jnp.exp2(aux_a - top)
+        wb = jnp.exp2(aux_b - top)
+        total = wa * sums_of(aux_a, local_heads) + wb * sums_of(aux_b, local_heads)
+        high, low = split(total)
+        is_top = (lane < local_heads) | (lane >= MOVED_LANE)
+        is_top = is_top & (lane < MOVED_LANE + local_heads) | (lane == TARGET_LANE)
+        high = pltpu.roll(high, local_heads, 1)
+        low = pltpu.roll(low, 2 * local_heads, 1)
+        part = lane % MOVED_LANE // local_heads
+        aux = jnp.where(is_top, top, jnp.where(part == 1, high, low))
+        parts = []
+        for j in range(local_heads + 1):
+            at = j if j < local_heads else MOVED_LANE
+            rows = slice(j * half_rs, (j + 1) * half_rs)
+            parts.append(wa[:, at : at + 1] * a[rows] + wb[:, at : at + 1] * b[rows])
+        out[h, k] = jnp.concatenate(parts + [aux], axis=0).astype(jnp.bfloat16)
+        return carry
+
+    lax.fori_loop(0, first.shape[0] * chips, one, 0, unroll=MERGE_UNROLL)
 
 
 def reduce_kernel(chips, steps, info, parts, out):

time: 57.3 us -> 55.7 us (0.972)
  Pallas kernels: 13.7 us -> 12.1 us
    pallas_call x1, Pallas kernels: 5.29 us -> 4.14 us  [per_device(): pl.pallas_call(lambda *refs: attend_kernel(chips, *refs), out_shape=(stat...]
where the time goes in v6:
time: 55.7 us; the launch traced here: 55.3 us
  blocking collectives  41 us (74%)
  Pallas kernels  12.1 us (22%)
  waiting for transfers between devices  1.59 us (3%)
  starting transfers between devices  0.58 us (1%)
    all_to_all x3, blocking collectives, exchange(): return lax.all_to_all(x, both, 0, 0, axis_index_groups=members)  41 us
    pallas_call x1, Pallas kernels, per_device(): pl.pallas_call(lambda *refs: attend_kernel(chips, *refs), out_shape=(stat...  4.14 us
    pallas_call x1, Pallas kernels, per_device(): pl.pallas_call(lambda *refs: prepare_kernel(steps, *refs), out_shape=(jax...  2.31 us
    pallas_call x1, Pallas kernels, per_device(): pl.pallas_call(lambda *refs: project_other_kernel(chips, *refs), out_shap...  1.81 us
    ppermute x1, waiting for transfers between devices, per_device(): lax.ppermute(send, 'tp', across)  1.43 us
    pallas_call x1, Pallas kernels, per_device(): pl.pallas_call(lambda *refs: project_own_kernel(chips, *refs), out_shape=...  1.19 us
  transfers between devices with their start and end apart: 4, of which 2 were waited for; matrix products, arithmetic and copies ran while one was open for 0% of the time, Pallas kernels for 6%

profile of v6, /device:TPU:0, one launch (start us, length us, event | category | flops | bytes accessed | tf_op | source)
XLA Modules:
  0.0 55.3 jit_solution(3090607871525578661)
XLA Ops:
  0.0 0.8 %pack.1 = (bf16[16,16,512]{2,1,0:T(8,128)(2,1)S(1)}, bf16[16,128]{1,0:T(8,128)(2,1)S(1)}) custom-call(bf16[8,2,512]{2,1,0:T(2,128)(2,1)} %bitcast.17, bf16[8,2,64]{2,1,0:T(2,128)(2,1)} %bitcast.18, bf16[8,2,64]{2,1,0:T(2,128)(2,1)} %bitcast.19), custom_call_target="tpu_custom_call" | custom-call | tf_op jit(solution)/shard_map/pack/pallas_call | solution.py:415
  0.8 18.0 %all_to_all.15.refs_5_.refs_2_ = bf16[16,16,512]{2,1,0:T(8,128)(2,1)S(1)} all-to-all(bf16[16,16,512]{2,1,0:T(8,128)(2,1)S(1)} %get-tuple-element.14), channel_id=1, replica_groups={{0,2,4,6,8,10,12,14,16,18,20,22,24,26,28,30},{1,3,5,7,9,11,13,15,17,19,..., dimensions={0} | all-to-all | bytes 524288 | tf_op jit(solution)/shard_map/all_to_all | solution.py:390
  18.8 0.0 collective-permute-start
  18.8 0.5 collective-permute-start.1
  19.4 0.1 pad_add_fusion.refs_0_
  19.4 0.0 copy-start
  19.4 2.3 %prepare.1 = (bf16[1024,1024]{1,0:T(8,128)(2,1)S(1)}, bf16[1024,1024]{1,0:T(8,128)(2,1)S(1)}, f32[16,1024]{1,0:T(8,128)S(1)}, f32[16,1024]{1,0:T(8,128)S(1)}) custom-call(s32[1,8]{1,0:T(1,128)} %refs_1_.3, s32[1,64]{1,0:T(1,128)} %refs_1_.2, s32[1,64]{1,0:T(1,128)} %refs_2_.1, bf16[1024,1024]{1,0:T(8,128)(2,1)} %bitcast.15, bf16[1024,1024]{1,0:T(8,128)(2,1)} %bitcast.16, ...), custom_call_target="tpu_custom_call" | custom-call | tf_op jit(solution)/shard_map/prepare/pallas_call | solution.py:441
  21.8 0.0 collective-permute-done.1.refs_10_
  21.8 0.0 collective-permute-done.refs_3_
  21.8 0.0 copy-done
  21.8 4.1 %attend.1 = (bf16[2,8,48,128]{3,2,1,0:T(8,128)(2,1)S(1)}, bf16[2,8,48,128]{3,2,1,0:T(8,128)(2,1)S(1)}, bf16[16,512,512]{2,1,0:T(8,128)(2,1)S(1)}) custom-call(s32[4]{0:T(128)S(1)} %pad_add_fusion.refs_0_, s32[1,8]{1,0:T(1,128)S(1)} %copy-done, bf16[16,16,512]{2,1,0:T(8,128)(2,1)S(1)} %all_to_all.15.refs_5_.refs_2_, ...), custom_call_target="tpu_custom_call" | custom-call | tf_op jit(solution)/shard_map/attend/pallas_call | solution.py:466
  25.9 0.1 collective-permute-start.2
  26.0 1.4 %collective-permute-done.2.refs_1_ = bf16[2,8,48,128]{3,2,1,0:T(8,128)(2,1)S(1)} collective-permute-done((bf16[2,8,48,128]{3,2,1,0:T(8,128)(2,1)S(1)}, bf16[2,8,48,128]{3,2,1,0:T(8,128)(2,1)S(1)}, u32[]{:S(2)}, u32[]{:S(2)}) %collective-permute-start.2) | collective-permute-done | bytes 196640 | tf_op jit(solution)/shard_map/ppermute | solution.py:497
  27.4 0.8 %merge.1 = bf16[2,8,48,128]{3,2,1,0:T(8,128)(2,1)S(1)} custom-call(bf16[2,8,48,128]{3,2,1,0:T(8,128)(2,1)S(1)} %get-tuple-element.20.refs_0_, bf16[2,8,48,128]{3,2,1,0:T(8,128)(2,1)S(1)} %collective-permute-done.2.refs_1_), custom_call_target="tpu_custom_call" | custom-call | tf_op jit(solution)/shard_map/merge/pallas_call | solution.py:490
  28.2 11.8 %all_to_all.16.refs_1_ = bf16[16,48,128]{2,1,0:T(8,128)(2,1)S(1)} all-to-all(bf16[16,48,128]{2,1,0:T(8,128)(2,1)S(1)} %bitcast.12), channel_id=1, replica_groups={{0,2,4,6,8,10,12,14,16,18,20,22,24,26,28,30},{1,3,5,7,9,11,13,15,17,19,..., dimensions={0} | all-to-all | bytes 393216 | tf_op jit(solution)/shard_map/all_to_all | solution.py:390
  40.0 1.0 %reduce.1 = bf16[2,8,8,512]{3,2,1,0:T(8,128)(2,1)S(1)} custom-call(s32[4]{0:T(128)S(1)} %pad_add_fusion.refs_0_, bf16[16,48,128]{2,1,0:T(8,128)(2,1)S(1)} %all_to_all.16.refs_1_), custom_call_target="tpu_custom_call" | custom-call | tf_op jit(solution)/shard_map/reduce/pallas_call | solution.py:499
  41.1 11.1 %all_to_all.17.refs_1_ = bf16[16,8,512]{2,1,0:T(8,128)(2,1)S(1)} all-to-all(bf16[16,8,512]{2,1,0:T(8,128)(2,1)S(1)} %bitcast.13), channel_id=1, replica_groups={{0,2,4,6,8,10,12,14,16,18,20,22,24,26,28,30},{1,3,5,7,9,11,13,15,17,19,..., dimensions={0} | all-to-all | bytes 262144 | tf_op jit(solution)/shard_map/all_to_all | solution.py:390
  52.2 0.0 collective-permute-start.3
  52.2 1.2 %project_own.1.refs_1_ = f32[16,512]{1,0:T(8,128)S(1)} custom-call(s32[4]{0:T(128)S(1)} %pad_add_fusion.refs_0_, bf16[16,8,512]{2,1,0:T(8,128)(2,1)S(1)} %all_to_all.17.refs_1_, bf16[16,512,512]{2,1,0:T(8,128)(2,1)S(1)} %get-tuple-element.22.refs_2_.refs_3_), custom_call_target="tpu_custom_call" | custom-call | tf_op jit(solution)/shard_map/project_own/pallas_call | solution.py:509
  53.4 0.2 collective-permute-done.3.refs_2_
  53.5 1.8 %project_other.1 = bf16[8,2,512]{2,1,0:T(2,128)(2,1)} custom-call(s32[4]{0:T(128)S(1)} %pad_add_fusion.refs_0_, f32[16,512]{1,0:T(8,128)S(1)} %project_own.1.refs_1_, bf16[16,8,512]{2,1,0:T(8,128)(2,1)S(1)} %collective-permute-done.3.refs_2_, bf16[16,512,512]{2,1,0:T(8,128)(2,1)S(1)} %get-tuple-element.22.refs_2_.refs_3_), custom_call_target="tpu_custom_call" | custom-call | tf_op jit(solution)/shard_map/project_other/pallas_call | solution.py:517
Async XLA Ops:
  18.8 2.9 %collective-permute-start = (bf16[16,16,512]{2,1,0:T(8,128)(2,1)S(1)}, bf16[16,16,512]{2,1,0:T(8,128)(2,1)S(1)}, u32[]{:S(2)}, u32[]{:S(2)}) collective-permute-start(bf16[16,16,512]{2,1,0:T(8,128)(2,1)S(1)} %all_to_all.15.refs_5_.refs_2_), channel_id=1, source_target_pairs={{0,1},{1,0},{2,3},{3,2},{4,5},{5,4},{6,7},{7,6},{8,9},{9,8},{10,11... | collective-permute-start | bytes 786440 | tf_op jit(solution)/shard_map/ppermute | solution.py:435
  18.8 2.9 %collective-permute-start.1 = (bf16[16,128]{1,0:T(8,128)(2,1)S(1)}, bf16[16,128]{1,0:T(8,128)(2,1)S(1)}, u32[]{:S(2)}, u32[]{:S(2)}) collective-permute-start(bf16[16,128]{1,0:T(8,128)(2,1)S(1)} %get-tuple-element.19.refs_9_), channel_id=1, source_target_pairs={{0,1},{1,0},{2,3},{3,2},{4,5},{5,4},{6,7},{7,6},{8,9},{9,8},{10,11... | collective-permute-start | bytes 12296 | tf_op jit(solution)/shard_map/ppermute | solution.py:431
  19.4 2.3 %copy-start = (s32[1,8]{1,0:T(1,128)S(1)}, s32[1,8]{1,0:T(1,128)}, u32[]{:S(2)}) copy-start(s32[1,8]{1,0:T(1,128)} %refs_1_.3) | copy-start | bytes 100
  25.9 1.5 %collective-permute-start.2 = (bf16[2,8,48,128]{3,2,1,0:T(8,128)(2,1)S(1)}, bf16[2,8,48,128]{3,2,1,0:T(8,128)(2,1)S(1)}, u32[]{:S(2)}, u32[]{:S(2)}) collective-permute-start(bf16[2,8,48,128]{3,2,1,0:T(8,128)(2,1)S(1)} %get-tuple-element.21), channel_id=1, source_target_pairs={{0,1},{1,0},{2,3},{3,2},{4,5},{5,4},{6,7},{7,6},{8,9},{9,8},{10,11... | collective-permute-start | bytes 589832 | tf_op jit(solution)/shard_map/ppermute | solution.py:497
  52.2 1.3 %collective-permute-start.3 = (bf16[16,8,512]{2,1,0:T(8,128)(2,1)S(1)}, bf16[16,8,512]{2,1,0:T(8,128)(2,1)S(1)}, u32[]{:S(2)}, u32[]{:S(2)}) collective-permute-start(bf16[16,8,512]{2,1,0:T(8,128)(2,1)S(1)} %all_to_all.17.refs_1_), channel_id=1, source_target_pairs={{0,1},{1,0},{2,3},{3,2},{4,5},{5,4},{6,7},{7,6},{8,9},{9,8},{10,11... | collective-permute-start | bytes 393224 | tf_op jit(solution)/shard_map/ppermute | solution.py:508
